TPU v7x, 32 devices: a whole 2x2x4 slice. The times are simulated.
32 devices in a mesh: row: 8 (over y, x, core), col: 4 (over z).
Axes of the slice: x: 2, y: 2, z: 4, core: 2. Of those that a mesh axis runs over, the one named last changes fastest.
Arguments:
- front_tiles: float32 [2, 2048, 2, 1024], P(None, 'row', None, 'col'), may hold values from -6 to 6, as said below
- lead_tiles: int32 [2, 8], P(None, 'row'), may hold values from 0 to 7
- damping: float32 [2, 1024], P(None, 'col'), may hold values from 1.5 to 6
Outputs:
- factor: float32 [2, 2048, 2, 1024], P(None, 'row', None, 'col')
Inputs may be any that keep to these rules, and one draw needn't show every extreme that they name: `front_tiles`: the front's entries. `lead_tiles`: entries of the first 8 tile rows are not read.
All inputs are finite; a program needn't handle non-finite values.
Results may differ from a plain program's by a relative error of at most 0.00005.
Values sent between devices are 32-bit elements; how exact they have to be, the bound alone decides.
No kernel may reach another device: no remote copies, remote signals or barrier semaphores. Data moves between devices by JAX's collectives and lax.ppermute only.
A program may use at most 64 MiB of HBM per device.

v0:
```python
import jax
import jax.numpy as jnp
from jax import lax
from jax.sharding import PartitionSpec as P


def from_root(value, axis, source):
    kept = jnp.where(lax.axis_index(axis) == source, value, 0).astype(value.dtype)
    return lax.psum(kept, axis)


def pick_tile(tiles, tile_rows, wanted):
    chosen = (tile_rows == wanted)[:, None, None]
    return jnp.sum(jnp.where(chosen, tiles, 0.0), axis=0)


def shards(front_tiles, lead_tiles, damping):
    slot_count, tile_size, col_slot_count, _ = front_tiles.shape
    n_row = lax.axis_size("row")
    n_col = lax.axis_size("col")
    row_at = lax.axis_index("row")
    col_at = lax.axis_index("col")
    n_columns = col_slot_count * n_col
    row_tiles = jnp.arange(slot_count, dtype=jnp.int32) * n_row + row_at
    col_tiles = jnp.arange(col_slot_count, dtype=jnp.int32) * n_col + col_at
    leads = jnp.where(row_tiles < n_columns, 0, lead_tiles[:, 0])
    working = front_tiles
    kept_mask = col_tiles[None, :] >= leads[:, None]
    working = jnp.where(kept_mask[:, None, :, None], working, 0.0)
    identity = jnp.eye(tile_size, dtype=jnp.float32)
    on_diagonal = (row_tiles[:, None] == col_tiles[None, :])[:, None, :, None]
    damp_term = identity[None, :, None, :] * damping[None, None, :, :]
    working = working + jnp.where(on_diagonal, damp_term, 0.0)
    for column in range(n_columns):
        owner_col = column % n_col
        col_slot = column // n_col
        column_panel = working[:, :, col_slot, :]
        diag_source = pick_tile(column_panel, row_tiles, column)
        diag_full = from_root(diag_source, "row", column % n_row)
        symmetric = jnp.tril(diag_full) + jnp.tril(diag_full, -1).T
        lower_factor = jnp.linalg.cholesky(symmetric)
        flattened = column_panel.reshape(slot_count * tile_size, tile_size)
        solved = jax.scipy.linalg.solve_triangular(lower_factor, flattened.T, lower=True).T
        solved = solved.reshape(slot_count, tile_size, tile_size)
        below = (row_tiles > column)[:, None, None]
        at_diag = (row_tiles == column)[:, None, None]
        new_panel = jnp.where(below, solved, jnp.where(at_diag, lower_factor[None], 0.0))
        is_owner = col_at == owner_col
        working = working.at[:, :, col_slot, :].set(jnp.where(is_owner, new_panel, column_panel))
        shared = from_root(new_panel, "col", owner_col)
        for target_slot in range(col_slot_count):
            target = col_tiles[target_slot]
            sep_source = pick_tile(shared, row_tiles, target)
            sep_tile = from_root(sep_source, "row", target)

            def apply_all(current):
                product_update = jnp.dot(
                    shared.reshape(slot_count * tile_size, tile_size),
                    sep_tile.T,
                    precision=lax.Precision.HIGHEST,
                    preferred_element_type=jnp.float32,
                )
                return current - product_update.reshape(slot_count, tile_size, tile_size)

            def keep_same(current):
                return current

            updated = lax.cond(target > column, apply_all, keep_same, working[:, :, target_slot, :])
            working = working.at[:, :, target_slot, :].set(updated)
    final_mask = kept_mask & (row_tiles[:, None] >= col_tiles[None, :])
    result = jnp.where(final_mask[:, None, :, None], working, 0.0)
    return result


def solution(mesh):
    in_specs = (P(None, "row", None, "col"), P(None, "row"), P(None, "col"))
    out_specs = P(None, "row", None, "col")
    return jax.shard_map(shards, mesh=mesh, in_specs=in_specs, out_specs=out_specs, check_vma=False)
```

profile of v0, /device:TPU:0, one launch (start us, length us, event | category | flops | bytes accessed | tf_op | source)
XLA Modules:
  0.0 1757.5 jit_solution(1839295650670124243)
XLA Ops:
  9.5 57.1 %all-reduce.34.cloned.1.call-done = f32[256,256]{1,0:T(8,128)} async-done(((f32[256,256]{1,0:T(8,128)}), f32[256,256]{1,0:T(8,128)}) %all-reduce.34.cloned.1.call-update) | async-done | bytes 262160 | tf_op jit(solution)/shard_map/psum | solution.py:9
  68.2 11.7 cholesky.382
  90.4 11.7 cholesky.399
  109.0 19.7 %custom-call.26 = f32[2,128,128]{1,2,0:T(8,128)S(1)} custom-call(f32[2,128,128]{2,1,0:T(8,128)S(1)} %get-tuple-element.649), custom_call_target="InvertDiagBlocksLowerTriangular" | custom-call | tf_op jit(solution)/shard_map/jit(_solve_triangular)/triangular_solve | solution.py:43
  135.7 33.3 %all-reduce.36.cloned.1.call-done = f32[2,256,256]{2,1,0:T(8,128)} async-done(((f32[2,256,256]{2,1,0:T(8,128)}), f32[2,256,256]{2,1,0:T(8,128)}) %all-reduce.36.cloned.1.call-update) | async-done | bytes 524304 | tf_op jit(solution)/shard_map/psum | solution.py:9
  171.9 55.2 %all-reduce.80.cloned.1.call-done = (f32[256,256]{1,0:T(8,128)}, f32[256,256]{1,0:T(8,128)}) async-done(((f32[256,256]{1,0:T(8,128)}, f32[256,256]{1,0:T(8,128)}), (f32[256,256]{1,0:T(8,128)}, f32[256,256]{1,0:T(8,128)})) %all-reduce.80.cloned.1.call-update) | async-done | bytes 524304 | tf_op jit(solution)/shard_map/psum | solution.py:9
  230.1 54.3 %all-reduce.38.cloned.1.call-done = f32[256,256]{1,0:T(8,128)} async-done(((f32[256,256]{1,0:T(8,128)}), f32[256,256]{1,0:T(8,128)}) %all-reduce.38.cloned.1.call-update) | async-done | bytes 262160 | tf_op jit(solution)/shard_map/psum | solution.py:9
  285.9 11.7 cholesky.416
  308.2 11.7 cholesky.433
  327.0 19.7 %custom-call.28 = f32[2,128,128]{1,2,0:T(8,128)S(1)} custom-call(f32[2,128,128]{2,1,0:T(8,128)S(1)} %get-tuple-element.650), custom_call_target="InvertDiagBlocksLowerTriangular" | custom-call | tf_op jit(solution)/shard_map/jit(_solve_triangular)/triangular_solve | solution.py:43
  350.5 36.5 %all-reduce.40.cloned.1.call-done = f32[2,256,256]{2,1,0:T(8,128)} async-done(((f32[2,256,256]{2,1,0:T(8,128)}), f32[2,256,256]{2,1,0:T(8,128)}) %all-reduce.40.cloned.1.call-update) | async-done | bytes 524304 | tf_op jit(solution)/shard_map/psum | solution.py:9
  390.0 55.0 %all-reduce.78.cloned.1.call-done = (f32[256,256]{1,0:T(8,128)}, f32[256,256]{1,0:T(8,128)}) async-done(((f32[256,256]{1,0:T(8,128)}, f32[256,256]{1,0:T(8,128)}), (f32[256,256]{1,0:T(8,128)}, f32[256,256]{1,0:T(8,128)})) %all-reduce.78.cloned.1.call-update) | async-done | bytes 524304 | tf_op jit(solution)/shard_map/psum | solution.py:9
  448.0 54.3 %all-reduce.42.cloned.1.call-done = f32[256,256]{1,0:T(8,128)} async-done(((f32[256,256]{1,0:T(8,128)}), f32[256,256]{1,0:T(8,128)}) %all-reduce.42.cloned.1.call-update) | async-done | bytes 262160 | tf_op jit(solution)/shard_map/psum | solution.py:9
  503.8 11.7 cholesky.450
  526.1 11.7 cholesky.467
  545.1 19.7 %custom-call.30 = f32[2,128,128]{1,2,0:T(8,128)S(1)} custom-call(f32[2,128,128]{2,1,0:T(8,128)S(1)} %get-tuple-element.651), custom_call_target="InvertDiagBlocksLowerTriangular" | custom-call | tf_op jit(solution)/shard_map/jit(_solve_triangular)/triangular_solve | solution.py:43
  568.6 36.5 %all-reduce.44.cloned.1.call-done = f32[2,256,256]{2,1,0:T(8,128)} async-done(((f32[2,256,256]{2,1,0:T(8,128)}), f32[2,256,256]{2,1,0:T(8,128)}) %all-reduce.44.cloned.1.call-update) | async-done | bytes 524304 | tf_op jit(solution)/shard_map/psum | solution.py:9
  608.1 55.2 %all-reduce.76.cloned.1.call-done = (f32[256,256]{1,0:T(8,128)}, f32[256,256]{1,0:T(8,128)}) async-done(((f32[256,256]{1,0:T(8,128)}, f32[256,256]{1,0:T(8,128)}), (f32[256,256]{1,0:T(8,128)}, f32[256,256]{1,0:T(8,128)})) %all-reduce.76.cloned.1.call-update) | async-done | bytes 524304 | tf_op jit(solution)/shard_map/psum | solution.py:9
  666.2 54.4 %all-reduce.46.cloned.1.call-done = f32[256,256]{1,0:T(8,128)} async-done(((f32[256,256]{1,0:T(8,128)}), f32[256,256]{1,0:T(8,128)}) %all-reduce.46.cloned.1.call-update) | async-done | bytes 262160 | tf_op jit(solution)/shard_map/psum | solution.py:9
  722.1 11.7 cholesky.484
  744.3 11.7 cholesky.501
  763.1 19.7 %custom-call.32 = f32[2,128,128]{1,2,0:T(8,128)S(1)} custom-call(f32[2,128,128]{2,1,0:T(8,128)S(1)} %get-tuple-element.652), custom_call_target="InvertDiagBlocksLowerTriangular" | custom-call | tf_op jit(solution)/shard_map/jit(_solve_triangular)/triangular_solve | solution.py:43
  786.7 36.4 %all-reduce.48.cloned.1.call-done = f32[2,256,256]{2,1,0:T(8,128)} async-done(((f32[2,256,256]{2,1,0:T(8,128)}), f32[2,256,256]{2,1,0:T(8,128)}) %all-reduce.48.cloned.1.call-update) | async-done | bytes 524304 | tf_op jit(solution)/shard_map/psum | solution.py:9
  826.1 55.0 %all-reduce.74.cloned.1.call-done = (f32[256,256]{1,0:T(8,128)}, f32[256,256]{1,0:T(8,128)}) async-done(((f32[256,256]{1,0:T(8,128)}, f32[256,256]{1,0:T(8,128)}), (f32[256,256]{1,0:T(8,128)}, f32[256,256]{1,0:T(8,128)})) %all-reduce.74.cloned.1.call-update) | async-done | bytes 524304 | tf_op jit(solution)/shard_map/psum | solution.py:9
  884.0 53.0 %all-reduce.50.cloned.1.call-done = f32[256,256]{1,0:T(8,128)} async-done(((f32[256,256]{1,0:T(8,128)}), f32[256,256]{1,0:T(8,128)}) %all-reduce.50.cloned.1.call-update) | async-done | bytes 262160 | tf_op jit(solution)/shard_map/psum | solution.py:9
  938.5 11.7 cholesky.518
  960.7 11.7 cholesky.535
  979.8 19.7 %custom-call.34 = f32[2,128,128]{1,2,0:T(8,128)S(1)} custom-call(f32[2,128,128]{2,1,0:T(8,128)S(1)} %get-tuple-element.653), custom_call_target="InvertDiagBlocksLowerTriangular" | custom-call | tf_op jit(solution)/shard_map/jit(_solve_triangular)/triangular_solve | solution.py:43
  1003.3 36.4 %all-reduce.52.cloned.1.call-done = f32[2,256,256]{2,1,0:T(8,128)} async-done(((f32[2,256,256]{2,1,0:T(8,128)}), f32[2,256,256]{2,1,0:T(8,128)}) %all-reduce.52.cloned.1.call-update) | async-done | bytes 524304 | tf_op jit(solution)/shard_map/psum | solution.py:9
  1042.7 55.0 %all-reduce.72.cloned.1.call-done = (f32[256,256]{1,0:T(8,128)}, f32[256,256]{1,0:T(8,128)}) async-done(((f32[256,256]{1,0:T(8,128)}, f32[256,256]{1,0:T(8,128)}), (f32[256,256]{1,0:T(8,128)}, f32[256,256]{1,0:T(8,128)})) %all-reduce.72.cloned.1.call-update) | async-done | bytes 524304 | tf_op jit(solution)/shard_map/psum | solution.py:9
  1099.8 53.6 %all-reduce.54.cloned.1.call-done = f32[256,256]{1,0:T(8,128)} async-done(((f32[256,256]{1,0:T(8,128)}), f32[256,256]{1,0:T(8,128)}) %all-reduce.54.cloned.1.call-update) | async-done | bytes 262160 | tf_op jit(solution)/shard_map/psum | solution.py:9
  1154.9 11.7 cholesky.552
  1177.2 11.7 cholesky.569
  1196.0 19.7 %custom-call.36 = f32[2,128,128]{1,2,0:T(8,128)S(1)} custom-call(f32[2,128,128]{2,1,0:T(8,128)S(1)} %get-tuple-element.654), custom_call_target="InvertDiagBlocksLowerTriangular" | custom-call | tf_op jit(solution)/shard_map/jit(_solve_triangular)/triangular_solve | solution.py:43
  1219.5 36.4 %all-reduce.56.cloned.1.call-done = f32[2,256,256]{2,1,0:T(8,128)} async-done(((f32[2,256,256]{2,1,0:T(8,128)}), f32[2,256,256]{2,1,0:T(8,128)}) %all-reduce.56.cloned.1.call-update) | async-done | bytes 524304 | tf_op jit(solution)/shard_map/psum | solution.py:9
  1258.9 55.0 %all-reduce.70.cloned.1.call-done = (f32[256,256]{1,0:T(8,128)}, f32[256,256]{1,0:T(8,128)}) async-done(((f32[256,256]{1,0:T(8,128)}, f32[256,256]{1,0:T(8,128)}), (f32[256,256]{1,0:T(8,128)}, f32[256,256]{1,0:T(8,128)})) %all-reduce.70.cloned.1.call-update) | async-done | bytes 524304 | tf_op jit(solution)/shard_map/psum | solution.py:9
  1316.2 53.6 %all-reduce.58.cloned.1.call-done = f32[256,256]{0,1:T(8,128)} async-done(((f32[256,256]{0,1:T(8,128)}), f32[256,256]{0,1:T(8,128)}) %all-reduce.58.cloned.1.call-update) | async-done | bytes 262160 | tf_op jit(solution)/shard_map/psum | solution.py:9
  1371.3 11.7 cholesky.586
  1393.6 11.7 cholesky.603
  1412.6 19.7 %custom-call.38 = f32[2,128,128]{1,2,0:T(8,128)S(1)} custom-call(f32[2,128,128]{2,1,0:T(8,128)S(1)} %get-tuple-element.655), custom_call_target="InvertDiagBlocksLowerTriangular" | custom-call | tf_op jit(solution)/shard_map/jit(_solve_triangular)/triangular_solve | solution.py:43
  1436.1 36.4 %all-reduce.60.cloned.1.call-done = f32[2,256,256]{2,1,0:T(8,128)} async-done(((f32[2,256,256]{2,1,0:T(8,128)}), f32[2,256,256]{2,1,0:T(8,128)}) %all-reduce.60.cloned.1.call-update) | async-done | bytes 524304 | tf_op jit(solution)/shard_map/psum | solution.py:9
  1475.5 55.1 %all-reduce.68.cloned.1.call-done = (f32[256,256]{1,0:T(8,128)}, f32[256,256]{1,0:T(8,128)}) async-done(((f32[256,256]{1,0:T(8,128)}, f32[256,256]{1,0:T(8,128)}), (f32[256,256]{1,0:T(8,128)}, f32[256,256]{1,0:T(8,128)})) %all-reduce.68.cloned.1.call-update) | async-done | bytes 524304 | tf_op jit(solution)/shard_map/psum | solution.py:9
  1533.0 53.5 %all-reduce.62.cloned.1.call-done = f32[256,256]{1,0:T(8,128)} async-done(((f32[256,256]{1,0:T(8,128)}), f32[256,256]{1,0:T(8,128)}) %all-reduce.62.cloned.1.call-update) | async-done | bytes 262160 | tf_op jit(solution)/shard_map/psum | solution.py:9
  1588.7 11.7 cholesky.620
  1610.8 11.7 cholesky.637
  1629.6 19.7 %custom-call.40 = f32[2,128,128]{1,2,0:T(8,128)S(1)} custom-call(f32[2,128,128]{2,1,0:T(8,128)S(1)} %get-tuple-element.656), custom_call_target="InvertDiagBlocksLowerTriangular" | custom-call | tf_op jit(solution)/shard_map/jit(_solve_triangular)/triangular_solve | solution.py:43
  1653.1 36.4 %all-reduce.64.cloned.1.call-done = f32[2,256,256]{2,1,0:T(8,128)} async-done(((f32[2,256,256]{2,1,0:T(8,128)}), f32[2,256,256]{2,1,0:T(8,128)}) %all-reduce.64.cloned.1.call-update) | async-done | bytes 524304 | tf_op jit(solution)/shard_map/psum | solution.py:9
  1692.5 55.0 %all-reduce.66.cloned.1.call-done = (f32[256,256]{1,0:T(8,128)}, f32[256,256]{1,0:T(8,128)}) async-done(((f32[256,256]{1,0:T(8,128)}, f32[256,256]{1,0:T(8,128)}), (f32[256,256]{1,0:T(8,128)}, f32[256,256]{1,0:T(8,128)})) %all-reduce.66.cloned.1.call-update) | async-done | bytes 524304 | tf_op jit(solution)/shard_map/psum | solution.py:9
  (477 shorter events, 247.0 us)
Async XLA Ops:
  6.5 1.6 copy-start.8
  6.5 60.1 %all-reduce.34.cloned.1.call-start = ((), (), s32[]{:S(2)}) async-start(), calls=%async_computation | async-start | bytes 524288 | tf_op jit(solution)/shard_map/psum | solution.py:9
  9.2 159.8 %all-reduce.36.cloned.1.call-start = ((), (), s32[]{:S(2)}) async-start(), calls=%async_computation.1 | async-start | bytes 1048576 | tf_op jit(solution)/shard_map/psum | solution.py:9
  66.7 1.2 copy-start.10
  131.1 96.0 %all-reduce.80.cloned.1.call-start = ((), (), s32[]{:S(2)}) async-start(), calls=%async_computation.23 | async-start | bytes 1048576 | tf_op jit(solution)/shard_map/psum | solution.py:9
  171.7 112.7 %all-reduce.38.cloned.1.call-start = ((), (), s32[]{:S(2)}) async-start(), calls=%async_computation.2 | async-start | bytes 524288 | tf_op jit(solution)/shard_map/psum | solution.py:9
  171.7 55.4 %copy-start = (f32[2,256,256]{2,1,0:T(8,128)S(1)}, f32[2,256,256]{2,1,0:T(8,128)}, u32[]{:S(2)}) copy-start(f32[2,256,256]{2,1,0:T(8,128)} %all-reduce.36.cloned.1.call-done) | copy-start | bytes 1572868
  227.1 1.0 copy-start.21
  229.8 157.2 %all-reduce.40.cloned.1.call-start = ((), (), s32[]{:S(2)}) async-start(), calls=%async_computation.3 | async-start | bytes 1048576 | tf_op jit(solution)/shard_map/psum | solution.py:9
  284.4 1.2 copy-start.12
  349.1 95.8 %all-reduce.78.cloned.1.call-start = ((), (), s32[]{:S(2)}) async-start(), calls=%async_computation.22 | async-start | bytes 1048576 | tf_op jit(solution)/shard_map/psum | solution.py:9
  389.7 112.6 %all-reduce.42.cloned.1.call-start = ((), (), s32[]{:S(2)}) async-start(), calls=%async_computation.4 | async-start | bytes 524288 | tf_op jit(solution)/shard_map/psum | solution.py:9
  389.8 55.2 %copy-start.7 = (f32[2,256,256]{2,1,0:T(8,128)S(1)}, f32[2,256,256]{2,1,0:T(8,128)}, u32[]{:S(2)}) copy-start(f32[2,256,256]{2,1,0:T(8,128)} %all-reduce.40.cloned.1.call-done) | copy-start | bytes 1572868
  445.0 1.0 copy-start.22
  447.6 157.4 %all-reduce.44.cloned.1.call-start = ((), (), s32[]{:S(2)}) async-start(), calls=%async_computation.5 | async-start | bytes 1048576 | tf_op jit(solution)/shard_map/psum | solution.py:9
  502.3 1.2 copy-start.13
  567.3 96.0 %all-reduce.76.cloned.1.call-start = ((), (), s32[]{:S(2)}) async-start(), calls=%async_computation.21 | async-start | bytes 1048576 | tf_op jit(solution)/shard_map/psum | solution.py:9
  607.8 112.7 %all-reduce.46.cloned.1.call-start = ((), (), s32[]{:S(2)}) async-start(), calls=%async_computation.6 | async-start | bytes 524288 | tf_op jit(solution)/shard_map/psum | solution.py:9
  607.9 55.4 %copy-start.5 = (f32[2,256,256]{2,1,0:T(8,128)S(1)}, f32[2,256,256]{2,1,0:T(8,128)}, u32[]{:S(2)}) copy-start(f32[2,256,256]{2,1,0:T(8,128)} %all-reduce.44.cloned.1.call-done) | copy-start | bytes 1572868
  663.3 1.0 copy-start.23
  665.9 157.2 %all-reduce.48.cloned.1.call-start = ((), (), s32[]{:S(2)}) async-start(), calls=%async_computation.7 | async-start | bytes 1048576 | tf_op jit(solution)/shard_map/psum | solution.py:9
  720.6 1.2 copy-start.11
  785.3 95.8 %all-reduce.74.cloned.1.call-start = ((), (), s32[]{:S(2)}) async-start(), calls=%async_computation.20 | async-start | bytes 1048576 | tf_op jit(solution)/shard_map/psum | solution.py:9
  825.8 111.1 %all-reduce.50.cloned.1.call-start = ((), (), s32[]{:S(2)}) async-start(), calls=%async_computation.8 | async-start | bytes 524288 | tf_op jit(solution)/shard_map/psum | solution.py:9
  825.9 55.2 %copy-start.6 = (f32[2,256,256]{2,1,0:T(8,128)S(1)}, f32[2,256,256]{2,1,0:T(8,128)}, u32[]{:S(2)}) copy-start(f32[2,256,256]{2,1,0:T(8,128)} %all-reduce.48.cloned.1.call-done) | copy-start | bytes 1572868
  881.1 1.0 copy-start.24
  883.7 156.0 %all-reduce.52.cloned.1.call-start = ((), (), s32[]{:S(2)}) async-start(), calls=%async_computation.9 | async-start | bytes 1048576 | tf_op jit(solution)/shard_map/psum | solution.py:9
  937.0 1.2 copy-start.14
  1001.9 95.8 %all-reduce.72.cloned.1.call-start = ((), (), s32[]{:S(2)}) async-start(), calls=%async_computation.19 | async-start | bytes 1048576 | tf_op jit(solution)/shard_map/psum | solution.py:9
  1042.4 111.0 %all-reduce.54.cloned.1.call-start = ((), (), s32[]{:S(2)}) async-start(), calls=%async_computation.10 | async-start | bytes 524288 | tf_op jit(solution)/shard_map/psum | solution.py:9
  1042.6 55.0 %copy-start.2 = (f32[2,256,256]{2,1,0:T(8,128)S(1)}, f32[2,256,256]{2,1,0:T(8,128)}, u32[]{:S(2)}) copy-start(f32[2,256,256]{2,1,0:T(8,128)} %all-reduce.52.cloned.1.call-done) | copy-start | bytes 1572868
  1097.7 1.0 copy-start.17
  1099.5 156.4 %all-reduce.56.cloned.1.call-start = ((), (), s32[]{:S(2)}) async-start(), calls=%async_computation.11 | async-start | bytes 1048576 | tf_op jit(solution)/shard_map/psum | solution.py:9
  1153.4 1.2 copy-start.15
  1218.1 95.8 %all-reduce.70.cloned.1.call-start = ((), (), s32[]{:S(2)}) async-start(), calls=%async_computation.18 | async-start | bytes 1048576 | tf_op jit(solution)/shard_map/psum | solution.py:9
  1258.7 111.1 %all-reduce.58.cloned.1.call-start = ((), (), s32[]{:S(2)}) async-start(), calls=%async_computation.12 | async-start | bytes 524288 | tf_op jit(solution)/shard_map/psum | solution.py:9
  1258.9 55.0 %copy-start.3 = (f32[2,256,256]{2,1,0:T(8,128)S(1)}, f32[2,256,256]{2,1,0:T(8,128)}, u32[]{:S(2)}) copy-start(f32[2,256,256]{2,1,0:T(8,128)} %all-reduce.56.cloned.1.call-done) | copy-start | bytes 1572868
  1314.0 1.0 copy-start.18
  1315.9 156.6 %all-reduce.60.cloned.1.call-start = ((), (), s32[]{:S(2)}) async-start(), calls=%async_computation.13 | async-start | bytes 1048576 | tf_op jit(solution)/shard_map/psum | solution.py:9
  1369.8 1.2 copy-start.16
  1434.7 96.0 %all-reduce.68.cloned.1.call-start = ((), (), s32[]{:S(2)}) async-start(), calls=%async_computation.17 | async-start | bytes 1048576 | tf_op jit(solution)/shard_map/psum | solution.py:9
  1475.3 111.3 %all-reduce.62.cloned.1.call-start = ((), (), s32[]{:S(2)}) async-start(), calls=%async_computation.14 | async-start | bytes 524288 | tf_op jit(solution)/shard_map/psum | solution.py:9
  1475.5 55.2 %copy-start.4 = (f32[2,256,256]{2,1,0:T(8,128)S(1)}, f32[2,256,256]{2,1,0:T(8,128)}, u32[]{:S(2)}) copy-start(f32[2,256,256]{2,1,0:T(8,128)} %all-reduce.60.cloned.1.call-done) | copy-start | bytes 1572868
  1530.7 1.0 copy-start.19
  1532.5 157.0 %all-reduce.64.cloned.1.call-start = ((), (), s32[]{:S(2)}) async-start(), calls=%async_computation.15 | async-start | bytes 1048576 | tf_op jit(solution)/shard_map/psum | solution.py:9
  1587.5 1.0 copy-start.9
  1651.7 95.8 %all-reduce.66.cloned.1.call-start = ((), (), s32[]{:S(2)}) async-start(), calls=%async_computation.16 | async-start | bytes 1048576 | tf_op jit(solution)/shard_map/psum | solution.py:9
  1692.4 55.1 %copy-start.1 = (f32[2,256,256]{2,1,0:T(8,128)S(1)}, f32[2,256,256]{2,1,0:T(8,128)}, u32[]{:S(2)}) copy-start(f32[2,256,256]{2,1,0:T(8,128)} %all-reduce.64.cloned.1.call-done) | copy-start | bytes 1572868
  (1 other events, 1.0 us)
Sparse Core Ops, SparseCore 0:
  10.4 56.2 all-reduce.33
  131.2 37.6 all-reduce.35
  172.4 54.6 all-reduce.79
  230.0 54.3 all-reduce.37
  349.3 37.6 all-reduce.39
  390.3 54.6 all-reduce.77
  448.0 54.2 all-reduce.41
  567.4 37.6 all-reduce.43
  608.5 54.6 all-reduce.75
  666.1 54.3 all-reduce.45
  785.4 37.6 all-reduce.47
  826.4 54.6 all-reduce.73
  884.1 52.7 all-reduce.49
  1002.0 37.6 all-reduce.51
  1043.0 54.6 all-reduce.71
  1100.6 52.7 all-reduce.53
  1218.2 37.6 all-reduce.55
  1259.2 54.6 all-reduce.69
  1317.0 52.7 all-reduce.57
  1434.8 37.6 all-reduce.59
  1476.0 54.6 all-reduce.67
  1533.7 52.7 all-reduce.61
  1651.8 37.6 all-reduce.63
  1692.8 54.6 all-reduce.65
where the time goes:
time: 1770 us; the launch traced here: 1760 us
  waiting for transfers between devices  1160 us (66%)
  other arithmetic  477 us (27%)
  local copies, waits for them, and re-layouts  58.3 us (3%)
  between operations  38.5 us (2%)
    psum x24, waiting for transfers between devices, from_root(): return lax.psum(kept, axis)  1160 us
    another operation x55, other arithmetic, shards(): lower_factor = jnp.linalg.cholesky(symmetric)  277 us
    another operation x17, other arithmetic, shards(): jax.scipy.linalg.solve_triangular(lower_factor, flattened.T, lower=True)  158 us
  transfers between devices with their start and end apart: 24, of which 24 were waited for; matrix products, arithmetic and copies ran while one was open for 0% of the time, Pallas kernels for 0%

commit v1 on v0

v1 whole, which is shorter than its diff:
```python
import jax
import jax.numpy as jnp
from jax import lax
from jax.sharding import PartitionSpec as P


def separator_tiles(sep_local, n_row, n_col, n_columns):
    sep_slots, tile, cslots, _ = sep_local.shape
    if sep_slots * n_row == n_columns:
        g = lax.all_gather(sep_local, ("row", "col"), axis=0)
        g = g.reshape(n_row, n_col, sep_slots, tile, cslots, tile)

        def get(i, j):
            return g[i % n_row, j % n_col, i // n_row, :, j // n_col, :]

        return get
    g = lax.all_gather(sep_local, "row", axis=1, tiled=True)
    g = g.reshape(sep_slots * n_row * tile, cslots, tile)[: n_columns * tile]
    g = lax.all_gather(g, "col", axis=2)

    def get(i, j):
        return g[i * tile:(i + 1) * tile, j // n_col, j % n_col, :]

    return get


def shards(front_tiles, lead_tiles, damping):
    slot_count, tile, col_slot_count, _ = front_tiles.shape
    n_row = lax.axis_size("row")
    n_col = lax.axis_size("col")
    row_at = lax.axis_index("row")
    col_at = lax.axis_index("col")
    n_columns = col_slot_count * n_col
    row_tiles = jnp.arange(slot_count, dtype=jnp.int32) * n_row + row_at
    col_tiles = jnp.arange(col_slot_count, dtype=jnp.int32) * n_col + col_at
    leads = jnp.where(row_tiles < n_columns, 0, lead_tiles[:, 0])
    kept_mask = col_tiles[None, :] >= leads[:, None]
    working = jnp.where(kept_mask[:, None, :, None], front_tiles, 0.0)

    sep_slots = -(-n_columns // n_row)
    get_tile = separator_tiles(working[:sep_slots], n_row, n_col, n_columns)
    damp_full = lax.all_gather(damping, "col", axis=1).reshape(n_columns, tile)

    tail_first = n_columns // n_row
    tail_slots = list(range(tail_first, slot_count))
    n_tail = len(tail_slots) * tile
    rows = lax.all_gather(working[tail_first:], "col", axis=3)
    rows = rows.reshape(n_tail, n_columns * tile)

    total_rows = n_columns * tile + n_tail
    factor = jnp.zeros((total_rows, n_columns * tile), jnp.float32)
    eye = jnp.eye(tile, dtype=jnp.float32)
    for k in range(n_columns):
        cols = slice(k * tile, (k + 1) * tile)
        diag = get_tile(k, k)
        diag = jnp.tril(diag) + jnp.tril(diag, -1).T + eye * damp_full[k][None, :]
        parts = [diag] + [get_tile(i, k) for i in range(k + 1, n_columns)] + [rows[:, cols]]
        panel = jnp.concatenate(parts, axis=0)
        if k > 0:
            left = factor[k * tile:, : k * tile]
            top = factor[k * tile:(k + 1) * tile, : k * tile]
            panel = panel - jnp.dot(left, top.T, precision=lax.Precision.HIGHEST,
                                    preferred_element_type=jnp.float32)
        lkk = jnp.tril(lax.linalg.cholesky(panel[:tile], symmetrize_input=True))
        below = lax.linalg.triangular_solve(lkk, panel[tile:], left_side=False, lower=True,
                                            transpose_a=True)
        factor = factor.at[k * tile:, cols].set(jnp.concatenate([lkk, below], axis=0))

    outs = []
    for slot in range(slot_count):
        tile_row = slot * n_row + row_at
        if slot < tail_first:
            start = tile_row * tile
        elif (slot + 1) * n_row <= n_columns:
            start = tile_row * tile
        else:
            tail_start = n_columns * tile + (slot - tail_first) * tile
            start = jnp.where(tile_row < n_columns, tile_row * tile, tail_start)
        picked = lax.dynamic_slice_in_dim(factor, start, tile, axis=0)
        picked = picked.reshape(tile, col_slot_count, n_col, tile)
        picked = lax.dynamic_index_in_dim(picked, col_at, axis=2, keepdims=False)
        outs.append(picked)
    return jnp.stack(outs, axis=0)


def solution(mesh):
    in_specs = (P(None, "row", None, "col"), P(None, "row"), P(None, "col"))
    out_specs = P(None, "row", None, "col")
    return jax.shard_map(shards, mesh=mesh, in_specs=in_specs, out_specs=out_specs, check_vma=False)
```

time: 1770 us -> 883 us (0.50)
  waiting for transfers between devices: 1160 us -> 147 us
  local copies, waits for them, and re-layouts: 58.3 us -> 148 us
  matrix products: 17 us -> 71.5 us
    psum x24 -> x0, waiting for transfers between devices: 1160 us -> none  [from_root(): return lax.psum(kept, axis)]
    all_gather x0 -> x2, waiting for transfers between devices: none -> 147 us  [the longest x1 115 us: separator_tiles(): g = lax.all_gather(sep_local, ('row', 'col'), axis=0)]
    unnamed x50 -> x152, local copies, waits for them, and re-layouts: 8.07 us -> 62 us
    dot_general x4 -> x7, matrix products: 3.04 us -> 43 us  [shards(): jnp.dot(left, top.T, precision=lax.Precision.HIGHEST, preferred_element_t...]
    select_n x34 -> x2, other arithmetic: 26.1 us -> 3.24 us  [the longest x1 1.86 us: shards(): diag = jnp.tril(diag) + jnp.tril(diag, -1).T + eye * damp_full[k][None, :]]
    another operation x95 -> x150, local copies, waits for them, and re-layouts: 35.6 us -> 53.5 us  [the longest x57 32.6 us: shards(): jax.scipy.linalg.solve_triangular(lower_factor, flattened.T, lower=True)]
    another operation x72 -> x76, other arithmetic: 434 us -> 444 us  [the longest x56 278 us: shards(): lkk = jnp.tril(lax.linalg.cholesky(panel[:tile], symmetrize_input=True))]
  transfers between devices with their start and end apart: 24 -> 2, of which waited for: 24 -> 2; matrix products, arithmetic and copies ran while one was open for 0% -> 1% of each run, Pallas kernels for 0% -> 0%
where the time goes in v1:
time: 883 us; the launch traced here: 871 us
  other arithmetic  465 us (53%)
  local copies, waits for them, and re-layouts  148 us (17%)
  waiting for transfers between devices  147 us (17%)
  matrix products  71.5 us (8%)
  between operations  26.1 us (3%)
  blocking collectives  13.6 us (2%)
    another operation x56, other arithmetic, shards(): lkk = jnp.tril(lax.linalg.cholesky(panel[:tile], symmetrize_input=True))  278 us
    another operation x17, other arithmetic, shards(): lax.linalg.triangular_solve(lkk, panel[tile:], left_side=False, lower=Tru...  164 us
    all_gather x1, waiting for transfers between devices, separator_tiles(): g = lax.all_gather(sep_local, ('row', 'col'), axis=0)  115 us
    unnamed x152, local copies, waits for them, and re-layouts  62 us
    another operation x80, local copies, waits for them, and re-layouts  46.8 us
    dot_general x7, matrix products, shards(): jnp.dot(left, top.T, precision=lax.Precision.HIGHEST, preferred_element_t...  43 us
    all_gather x1, waiting for transfers between devices, shards(): rows = lax.all_gather(working[tail_first:], 'col', axis=3)  31.9 us
    another operation x24, matrix products, shards(): lax.linalg.triangular_solve(lkk, panel[tile:], left_side=False, lower=Tru...  20.9 us
  transfers between devices with their start and end apart: 2, of which 2 were waited for; matrix products, arithmetic and copies ran while one was open for 1% of the time, Pallas kernels for 0%

profile of v1, /device:TPU:0, one launch (start us, length us, event | category | flops | bytes accessed | tf_op | source)
XLA Modules:
  0.0 871.4 jit_solution(2046340784994327779)
XLA Ops:
  10.5 13.6 %all-gather.1 = f32[2,1024]{1,0:T(2,128)S(1)} all-gather(f32[2,256]{1,0:T(2,128)S(1)} %copy-done.47), channel_id=3, replica_groups=mesh['row'=8,'col'=4] {'col'}, dimensions={1}, use_global_device_ids=true | all-gather | bytes 10240 | tf_op jit(solution)/shard_map/all_gather | solution.py:42
  26.6 31.9 %all-gather.8.cloned.1.call-done = f32[1,256,2,1024]{3,1,2,0:T(8,128)} async-done(((f32[1,256,2,256]{3,1,2,0:T(8,128)}), f32[1,256,2,1024]{3,1,2,0:T(8,128)}) %all-gather.8.cloned.1.call-update) | async-done | bytes 2097168 | tf_op jit(solution)/shard_map/all_gather | solution.py:47
  60.5 114.8 %all-gather.6.cloned.1.call-done = f32[32,256,2,256]{3,1,2,0:T(8,128)} async-done(((f32[1,256,2,256]{3,1,2,0:T(8,128)}), f32[32,256,2,256]{3,1,2,0:T(8,128)}) %all-gather.6.cloned.1.call-update) | async-done | bytes 16777232 | tf_op jit(solution)/shard_map/all_gather | solution.py:10
  187.9 11.7 %custom-call.63 = f32[128,128]{1,0:T(8,128)S(1)} custom-call(f32[128,128]{1,0:T(8,128)S(1)} %copy.377), custom_call_target="Cholesky" | custom-call | tf_op jit(solution)/shard_map/cholesky/custom-call.2 | solution.py:64
  199.6 9.8 %custom-call.64 = f32[1,128,128]{1,2,0:T(8,128)S(1)} custom-call(f32[1,128,128]{2,1,0:T(8,128)S(1)} %get-tuple-element.455), custom_call_target="InvertDiagBlocksLowerTriangular" | custom-call | tf_op jit(solution)/shard_map/cholesky/custom-call.11 | solution.py:64
  211.8 11.7 %custom-call.65 = f32[128,128]{1,0:T(8,128)S(1)} custom-call(f32[128,128]{1,0:T(8,128)S(1)} %copy.379), custom_call_target="Cholesky" | custom-call | tf_op jit(solution)/shard_map/cholesky/custom-call.3 | solution.py:64
  235.4 6.5 while.16
  241.8 21.4 %custom-call.34 = f32[2,128,128]{1,2,0:T(8,128)} custom-call(f32[2,128,128]{2,1,0:T(8,128)} %get-tuple-element.109), custom_call_target="InvertDiagBlocksLowerTriangular" | custom-call | tf_op jit(solution)/shard_map/triangular_solve | solution.py:65
  336.7 11.9 %custom-call.66 = f32[128,128]{1,0:T(8,128)S(1)} custom-call(f32[128,128]{1,0:T(8,128)S(1)} %copy.398), custom_call_target="Cholesky" | custom-call | tf_op jit(solution)/shard_map/cholesky/custom-call.2 | solution.py:64
  348.6 9.8 %custom-call.67 = f32[1,128,128]{1,2,0:T(8,128)S(1)} custom-call(f32[1,128,128]{2,1,0:T(8,128)S(1)} %get-tuple-element.453), custom_call_target="InvertDiagBlocksLowerTriangular" | custom-call | tf_op jit(solution)/shard_map/cholesky/custom-call.11 | solution.py:64
  360.8 11.7 %custom-call.68 = f32[128,128]{1,0:T(8,128)S(1)} custom-call(f32[128,128]{1,0:T(8,128)S(1)} %copy.400), custom_call_target="Cholesky" | custom-call | tf_op jit(solution)/shard_map/cholesky/custom-call.3 | solution.py:64
  377.0 6.9 while.17
  383.9 20.9 %custom-call.35 = f32[2,128,128]{1,2,0:T(8,128)S(1)} custom-call(f32[2,128,128]{2,1,0:T(8,128)} %get-tuple-element.117), custom_call_target="InvertDiagBlocksLowerTriangular" | custom-call | tf_op jit(solution)/shard_map/triangular_solve | solution.py:65
  410.0 7.7 scatter.26
  425.7 11.7 %custom-call.69 = f32[128,128]{1,0:T(8,128)S(1)} custom-call(f32[128,128]{1,0:T(8,128)S(1)} %copy.417), custom_call_target="Cholesky" | custom-call | tf_op jit(solution)/shard_map/cholesky/custom-call.2 | solution.py:64
  437.5 9.9 %custom-call.70 = f32[1,128,128]{1,2,0:T(8,128)S(1)} custom-call(f32[1,128,128]{2,1,0:T(8,128)S(1)} %get-tuple-element.451), custom_call_target="InvertDiagBlocksLowerTriangular" | custom-call | tf_op jit(solution)/shard_map/cholesky/custom-call.11 | solution.py:64
  448.1 11.7 %custom-call.71 = f32[128,128]{1,0:T(8,128)S(1)} custom-call(f32[128,128]{1,0:T(8,128)S(1)} %copy.419), custom_call_target="Cholesky" | custom-call | tf_op jit(solution)/shard_map/cholesky/custom-call.3 | solution.py:64
  463.0 5.7 while.18
  468.7 19.7 %custom-call.36 = f32[2,128,128]{1,2,0:T(8,128)S(1)} custom-call(f32[2,128,128]{2,1,0:T(8,128)S(1)} %get-tuple-element.125), custom_call_target="InvertDiagBlocksLowerTriangular" | custom-call | tf_op jit(solution)/shard_map/triangular_solve | solution.py:65
  493.0 6.9 fusion.15
  500.2 11.7 %custom-call.72 = f32[128,128]{1,0:T(8,128)S(1)} custom-call(f32[128,128]{1,0:T(8,128)S(1)} %copy.435), custom_call_target="Cholesky" | custom-call | tf_op jit(solution)/shard_map/cholesky/custom-call.2 | solution.py:64
  511.9 9.8 %custom-call.73 = f32[1,128,128]{1,2,0:T(8,128)S(1)} custom-call(f32[1,128,128]{2,1,0:T(8,128)S(1)} %get-tuple-element.449), custom_call_target="InvertDiagBlocksLowerTriangular" | custom-call | tf_op jit(solution)/shard_map/cholesky/custom-call.11 | solution.py:64
  522.4 11.7 %custom-call.74 = f32[128,128]{1,0:T(8,128)S(1)} custom-call(f32[128,128]{1,0:T(8,128)S(1)} %copy.437), custom_call_target="Cholesky" | custom-call | tf_op jit(solution)/shard_map/cholesky/custom-call.3 | solution.py:64
  537.3 5.7 while.19
  543.0 19.9 %custom-call.37 = f32[2,128,128]{1,2,0:T(8,128)S(1)} custom-call(f32[2,128,128]{2,1,0:T(8,128)S(1)} %get-tuple-element.133), custom_call_target="InvertDiagBlocksLowerTriangular" | custom-call | tf_op jit(solution)/shard_map/triangular_solve | solution.py:65
  566.5 7.6 fusion.12
  574.4 11.7 %custom-call.75 = f32[128,128]{1,0:T(8,128)S(1)} custom-call(f32[128,128]{1,0:T(8,128)S(1)} %copy.452), custom_call_target="Cholesky" | custom-call | tf_op jit(solution)/shard_map/cholesky/custom-call.2 | solution.py:64
  586.2 10.2 %custom-call.76 = f32[1,128,128]{1,2,0:T(8,128)S(1)} custom-call(f32[1,128,128]{2,1,0:T(8,128)S(1)} %get-tuple-element.447), custom_call_target="InvertDiagBlocksLowerTriangular" | custom-call | tf_op jit(solution)/shard_map/cholesky/custom-call.11 | solution.py:64
  597.0 11.7 %custom-call.77 = f32[128,128]{1,0:T(8,128)S(1)} custom-call(f32[128,128]{1,0:T(8,128)S(1)} %copy.454), custom_call_target="Cholesky" | custom-call | tf_op jit(solution)/shard_map/cholesky/custom-call.3 | solution.py:64
  612.6 5.7 while.20
  618.3 19.7 %custom-call.38 = f32[2,128,128]{1,2,0:T(8,128)S(1)} custom-call(f32[2,128,128]{2,1,0:T(8,128)S(1)} %get-tuple-element.141), custom_call_target="InvertDiagBlocksLowerTriangular" | custom-call | tf_op jit(solution)/shard_map/triangular_solve | solution.py:65
  642.8 7.7 fusion.24
  650.9 11.7 %custom-call.78 = f32[128,128]{1,0:T(8,128)S(1)} custom-call(f32[128,128]{1,0:T(8,128)S(1)} %copy.469), custom_call_target="Cholesky" | custom-call | tf_op jit(solution)/shard_map/cholesky/custom-call.2 | solution.py:64
  662.7 9.8 %custom-call.79 = f32[1,128,128]{1,2,0:T(8,128)S(1)} custom-call(f32[1,128,128]{2,1,0:T(8,128)S(1)} %get-tuple-element.445), custom_call_target="InvertDiagBlocksLowerTriangular" | custom-call | tf_op jit(solution)/shard_map/cholesky/custom-call.11 | solution.py:64
  673.1 11.7 %custom-call.80 = f32[128,128]{1,0:T(8,128)S(1)} custom-call(f32[128,128]{1,0:T(8,128)S(1)} %copy.471), custom_call_target="Cholesky" | custom-call | tf_op jit(solution)/shard_map/cholesky/custom-call.3 | solution.py:64
  688.0 5.7 while.21
  693.7 20.1 %custom-call.39 = f32[2,128,128]{1,2,0:T(8,128)S(1)} custom-call(f32[2,128,128]{2,1,0:T(8,128)S(1)} %get-tuple-element.149), custom_call_target="InvertDiagBlocksLowerTriangular" | custom-call | tf_op jit(solution)/shard_map/triangular_solve | solution.py:65
  716.6 7.1 fusion.28
  724.0 11.7 %custom-call.81 = f32[128,128]{1,0:T(8,128)S(1)} custom-call(f32[128,128]{1,0:T(8,128)S(1)} %slice.806), custom_call_target="Cholesky" | custom-call | tf_op jit(solution)/shard_map/cholesky/custom-call.2 | solution.py:64
  735.7 10.0 %custom-call.82 = f32[1,128,128]{1,2,0:T(8,128)S(1)} custom-call(f32[1,128,128]{2,1,0:T(8,128)S(1)} %get-tuple-element.443), custom_call_target="InvertDiagBlocksLowerTriangular" | custom-call | tf_op jit(solution)/shard_map/cholesky/custom-call.11 | solution.py:64
  746.2 11.7 %custom-call.83 = f32[128,128]{1,0:T(8,128)S(1)} custom-call(f32[128,128]{1,0:T(8,128)S(1)} %convolution_subtract_fusion.10), custom_call_target="Cholesky" | custom-call | tf_op jit(solution)/shard_map/cholesky/custom-call.3 | solution.py:64
  761.0 5.6 while.22
  766.7 19.7 %custom-call.40 = f32[2,128,128]{1,2,0:T(8,128)S(1)} custom-call(f32[2,128,128]{2,1,0:T(8,128)S(1)} %get-tuple-element.157), custom_call_target="InvertDiagBlocksLowerTriangular" | custom-call | tf_op jit(solution)/shard_map/triangular_solve | solution.py:65
  788.6 6.0 fusion.33
  795.0 11.7 %custom-call.84 = f32[128,128]{1,0:T(8,128)S(1)} custom-call(f32[128,128]{1,0:T(8,128)S(1)} %slice.815), custom_call_target="Cholesky" | custom-call | tf_op jit(solution)/shard_map/cholesky/custom-call.2 | solution.py:64
  806.7 9.8 %custom-call.85 = f32[1,128,128]{1,2,0:T(8,128)S(1)} custom-call(f32[1,128,128]{2,1,0:T(8,128)S(1)} %get-tuple-element.441), custom_call_target="InvertDiagBlocksLowerTriangular" | custom-call | tf_op jit(solution)/shard_map/cholesky/custom-call.11 | solution.py:64
  817.0 11.9 %custom-call.86 = f32[128,128]{1,0:T(8,128)S(1)} custom-call(f32[128,128]{1,0:T(8,128)S(1)} %convolution_subtract_fusion.9), custom_call_target="Cholesky" | custom-call | tf_op jit(solution)/shard_map/cholesky/custom-call.3 | solution.py:64
  837.7 19.7 %custom-call.41 = f32[2,128,128]{1,2,0:T(8,128)S(1)} custom-call(f32[2,128,128]{2,1,0:T(8,128)S(1)} %get-tuple-element.165), custom_call_target="InvertDiagBlocksLowerTriangular" | custom-call | tf_op jit(solution)/shard_map/triangular_solve | solution.py:65
  (452 shorter events, 219.3 us)
Async XLA Ops:
  6.5 52.0 %all-gather.8.cloned.1.call-start = ((), (), s32[]{:S(2)}) async-start(), calls=%async_computation.1 | async-start | bytes 2621440 | tf_op jit(solution)/shard_map/all_gather | solution.py:47
  8.7 1.8 copy-start.47
  9.7 165.5 %all-gather.6.cloned.1.call-start = ((), (), s32[]{:S(2)}) async-start(), calls=%async_computation | async-start | bytes 17301504 | tf_op jit(solution)/shard_map/all_gather | solution.py:10
  26.0 154.5 %copy-start.45 = (s32[256]{0:T(256)}, s32[256]{0:T(256)S(1)}, u32[]{:S(2)}) copy-start(s32[256]{0:T(256)S(1)} %iota_add_fusion) | copy-start | bytes 3076
  241.8 29.8 %copy-start.41 = (pred[256,256]{1,0:T(8,128)(4,1)S(1)}, pred[256,256]{1,0:T(8,128)(4,1)}, u32[]{:S(2)}) copy-start(pred[256,256]{1,0:T(8,128)(4,1)} %copy.460) | copy-start | bytes 196612
  283.3 12.6 %copy-start.16 = (f32[1,1,1,256,1,256]{5,3,4,2,1,0:T(8,128)S(1)}, f32[1,1,1,256,1,256]{5,3,4,2,1,0:T(8,128)}, u32[]{:S(2)}) copy-start(f32[1,1,1,256,1,256]{5,3,4,2,1,0:T(8,128)} %get-tuple-element.408) | copy-start | bytes 786436
  296.7 11.6 %copy-start.15 = (f32[1,1,1,256,1,256]{5,3,4,2,1,0:T(8,128)S(1)}, f32[1,1,1,256,1,256]{5,3,4,2,1,0:T(8,128)}, u32[]{:S(2)}) copy-start(f32[1,1,1,256,1,256]{5,3,4,2,1,0:T(8,128)} %get-tuple-element.417) | copy-start | bytes 786436
  298.6 9.8 %copy-start.43 = (f32[1,256]{1,0:T(1,128)S(1)}, f32[1,256]{1,0:T(1,128)}, u32[]{:S(2)}) copy-start(f32[1,256]{1,0:T(1,128)} %get-tuple-element.460) | copy-start | bytes 3076
  298.6 9.9 %copy-start.44 = (f32[1,256]{1,0:T(1,128)S(1)}, f32[1,256]{1,0:T(1,128)}, u32[]{:S(2)}) copy-start(f32[1,256]{1,0:T(1,128)} %get-tuple-element.461) | copy-start | bytes 3076
  298.6 9.9 %copy-start.46 = (s32[256]{0:T(256)S(1)}, s32[256]{0:T(256)}, u32[]{:S(2)}) copy-start(s32[256]{0:T(256)} %copy-done.45) | copy-start | bytes 3076
  304.8 3.6 copy-start.17
  308.4 2.9 copy-start.36
  308.5 2.9 copy-start.35
  308.5 3.0 copy-start.34
  308.5 3.0 copy-start.33
  311.3 0.9 copy-start.32
  311.3 1.0 copy-start.37
  311.3 1.1 copy-start.38
  311.3 1.2 copy-start.30
  311.3 1.2 copy-start.28
  311.4 1.3 copy-start.27
  311.4 1.3 copy-start.26
  311.5 1.4 copy-start.25
  312.3 1.1 copy-start.23
  312.4 1.7 copy-start.24
  312.5 2.4 copy-start.22
  312.5 3.1 copy-start.21
  317.1 5.5 copy-start.42
  318.1 1.3 copy-start.3
  319.4 1.2 copy-start.5
  320.6 1.2 copy-start.7
  322.6 2.5 copy-start.2
  325.1 2.9 copy-start.20
  328.0 1.6 copy-start.1
  331.7 1.4 copy-start
  410.0 7.7 copy-start.31
  417.7 2.1 copy-start.4
  490.9 2.1 copy-start.6
  564.3 2.2 copy-start.8
  618.3 21.6 %copy-start.14 = (f32[1,1,1,256,1,256]{5,3,4,2,1,0:T(8,128)S(1)}, f32[1,1,1,256,1,256]{5,3,4,2,1,0:T(8,128)}, u32[]{:S(2)}) copy-start(f32[1,1,1,256,1,256]{5,3,4,2,1,0:T(8,128)} %get-tuple-element.401) | copy-start | bytes 786436
  638.0 2.8 copy-start.13
  639.3 2.4 copy-start.29
  639.9 2.9 copy-start.10
  639.9 2.9 copy-start.11
  640.8 2.1 copy-start.18
  641.6 1.2 copy-start.19
  688.0 27.4 %copy-start.12 = (f32[256,256]{1,0:T(8,128)S(1)}, f32[256,256]{1,0:T(8,128)}, u32[]{:S(2)}) copy-start(f32[256,256]{1,0:T(8,128)} %get-tuple-element.426) | copy-start | bytes 786436
  714.3 2.4 copy-start.9
  (2 other events, 1.4 us)
Sparse Core Ops, SparseCore 0:
  9.9 48.6 all-gather.7
  61.5 113.6 all-gather.5

commit v2 on v1

v2 whole, which is shorter than its diff:
```python
import jax
import jax.numpy as jnp
from jax import lax
from jax.sharding import PartitionSpec as P

HIGHEST = lax.Precision.HIGHEST


def mm(a, b):
    return jnp.dot(a, b, precision=HIGHEST, preferred_element_type=jnp.float32)


def separator_tiles(sep_local, n_row, n_col, n_columns):
    sep_slots, tile, cslots, _ = sep_local.shape
    if sep_slots * n_row == n_columns:
        pieces = [lax.all_gather(sep_local[:, :, t, :], ("row", "col"), axis=0)
                  for t in range(cslots)]

        def get(i, j):
            g = pieces[j // n_col]
            return g[(i % n_row) * n_col + j % n_col, i // n_row]

        return get
    g = lax.all_gather(sep_local, "row", axis=1, tiled=True)
    g = g.reshape(sep_slots * n_row * tile, cslots, tile)[: n_columns * tile]
    g = lax.all_gather(g, "col", axis=2)

    def get(i, j):
        return g[i * tile:(i + 1) * tile, j // n_col, j % n_col, :]

    return get


def lower_inverse(lower):
    eye = jnp.eye(lower.shape[0], dtype=lower.dtype)
    return lax.linalg.triangular_solve(lower, eye, left_side=True, lower=True)


def factor_diag(diag):
    half = diag.shape[0] // 2
    l00 = jnp.tril(lax.linalg.cholesky(diag[:half, :half], symmetrize_input=False))
    i00 = lower_inverse(l00)
    l10 = mm(diag[half:, :half], i00.T)
    s11 = diag[half:, half:] - mm(l10, l10.T)
    l11 = jnp.tril(lax.linalg.cholesky(s11, symmetrize_input=True))
    i11 = lower_inverse(l11)
    i10 = -mm(i11, mm(l10, i00))
    zero = jnp.zeros((half, half), diag.dtype)
    lkk = jnp.block([[l00, zero], [l10, l11]])
    linv = jnp.block([[i00, zero], [i10, i11]])
    return lkk, linv


def shards(front_tiles, lead_tiles, damping):
    slot_count, tile, col_slot_count, _ = front_tiles.shape
    n_row = lax.axis_size("row")
    n_col = lax.axis_size("col")
    row_at = lax.axis_index("row")
    col_at = lax.axis_index("col")
    n_columns = col_slot_count * n_col
    row_tiles = jnp.arange(slot_count, dtype=jnp.int32) * n_row + row_at
    col_tiles = jnp.arange(col_slot_count, dtype=jnp.int32) * n_col + col_at
    leads = jnp.where(row_tiles < n_columns, 0, lead_tiles[:, 0])
    kept_mask = col_tiles[None, :] >= leads[:, None]
    working = jnp.where(kept_mask[:, None, :, None], front_tiles, 0.0)
    identity = jnp.eye(tile, dtype=jnp.float32)
    on_diagonal = (row_tiles[:, None] == col_tiles[None, :])[:, None, :, None]
    damp_term = identity[None, :, None, :] * damping[None, None, :, :]
    working = working + jnp.where(on_diagonal, damp_term, 0.0)

    sep_slots = -(-n_columns // n_row)
    get_tile = separator_tiles(working[:sep_slots], n_row, n_col, n_columns)

    tail_first = n_columns // n_row
    n_tail = (slot_count - tail_first) * tile
    tail_pieces = [lax.all_gather(working[tail_first:, :, t, :], "col", axis=2).reshape(n_tail, n_col * tile)
                   for t in range(col_slot_count)]

    total_rows = n_columns * tile + n_tail
    factor = jnp.zeros((total_rows, n_columns * tile), jnp.float32)
    for k in range(n_columns):
        cols = slice(k * tile, (k + 1) * tile)
        local = slice((k % n_col) * tile, (k % n_col + 1) * tile)
        parts = [get_tile(i, k) for i in range(k, n_columns)] + [tail_pieces[k // n_col][:, local]]
        panel = jnp.concatenate(parts, axis=0)
        if k > 0:
            left = factor[k * tile:, : k * tile]
            top = factor[k * tile:(k + 1) * tile, : k * tile]
            panel = panel - mm(left, top.T)
        diag = panel[:tile]
        diag = jnp.tril(diag) + jnp.tril(diag, -1).T
        lkk, linv = factor_diag(diag)
        below = mm(panel[tile:], linv.T)
        factor = factor.at[k * tile:, cols].set(jnp.concatenate([lkk, below], axis=0))

    outs = []
    for slot in range(slot_count):
        tile_row = slot * n_row + row_at
        if slot < tail_first:
            start = tile_row * tile
        else:
            tail_start = n_columns * tile + (slot - tail_first) * tile
            start = jnp.where(tile_row < n_columns, tile_row * tile, tail_start)
        picked = lax.dynamic_slice_in_dim(factor, start, tile, axis=0)
        picked = picked.reshape(tile, col_slot_count, n_col, tile)
        picked = lax.dynamic_index_in_dim(picked, col_at, axis=2, keepdims=False)
        outs.append(picked)
    return jnp.stack(outs, axis=0)


def solution(mesh):
    in_specs = (P(None, "row", None, "col"), P(None, "row"), P(None, "col"))
    out_specs = P(None, "row", None, "col")
    return jax.shard_map(shards, mesh=mesh, in_specs=in_specs, out_specs=out_specs, check_vma=False)
```

time: 883 us -> 769 us (0.87)
  other arithmetic: 465 us -> 395 us
  local copies, waits for them, and re-layouts: 148 us -> 130 us
  blocking collectives: 13.6 us -> 0 us
  waiting for transfers between devices: 147 us -> 135 us
  between operations: 26.1 us -> 15.2 us
  matrix products: 71.5 us -> 81 us
    another operation x75 -> x82, other arithmetic: 444 us -> 379 us  [the longest x32 175 us: lower_inverse(): return lax.linalg.triangular_solve(lower, eye, left_side=True, lower=True)]
    another operation x149 -> x8, local copies, waits for them, and re-layouts: 51.7 us -> 3.43 us  [lower_inverse(): return lax.linalg.triangular_solve(lower, eye, left_side=True, lower=True)]
    dot_general x7 -> x47, matrix products: 43 us -> 74.3 us  [mm(): return jnp.dot(a, b, precision=HIGHEST, preferred_element_type=jnp.float32)]
    another operation x40 -> x16, matrix products: 28.5 us -> 6.7 us  [lower_inverse(): return lax.linalg.triangular_solve(lower, eye, left_side=True, lower=True)]
    unnamed x152 -> x155, local copies, waits for them, and re-layouts: 62 us -> 78.9 us
    all_gather x1 -> x0, blocking collectives: 13.6 us -> none  [shards(): damp_full = lax.all_gather(damping, 'col', axis=1).reshape(n_columns, tile)]
    all_gather x2 -> x4, waiting for transfers between devices: 147 us -> 133 us  [the longest x2 78.3 us: separator_tiles(): lax.all_gather(sep_local[:, :, t, :], ('row', 'col'), axis=0)]
    slice x17 -> x33, local copies, waits for them, and re-layouts: 5.33 us -> 15.9 us  [the longest x3 9.97 us: get(): return g[i % n_row * n_col + j % n_col, i // n_row]]
  transfers between devices with their start and end apart: 2 -> 4, of which waited for: 2 -> 3; matrix products, arithmetic and copies ran while one was open for 1% -> 44% of each run, Pallas kernels for 0% -> 0%
where the time goes in v2:
time: 769 us; the launch traced here: 757 us
  other arithmetic  395 us (51%)
  waiting for transfers between devices  135 us (18%)
  local copies, waits for them, and re-layouts  130 us (17%)
  matrix products  81 us (11%)
  between operations  15.2 us (2%)
    another operation x32, other arithmetic, lower_inverse(): return lax.linalg.triangular_solve(lower, eye, left_side=True, lower=True)  175 us
    another operation x24, other arithmetic, factor_diag(): l11 = jnp.tril(lax.linalg.cholesky(s11, symmetrize_input=True))  102 us
    another operation x24, other arithmetic, factor_diag(): lax.linalg.cholesky(diag[:half, :half], symmetrize_input=False)  100 us
    unnamed x155, local copies, waits for them, and re-layouts  78.9 us
    all_gather x2, waiting for transfers between devices, separator_tiles(): lax.all_gather(sep_local[:, :, t, :], ('row', 'col'), axis=0)  78.3 us
    dot_general x47, matrix products, mm(): return jnp.dot(a, b, precision=HIGHEST, preferred_element_type=jnp.float32)  74.3 us
    all_gather x2, waiting for transfers between devices, shards(): lax.all_gather(working[tail_first:, :, t, :], 'col', axis=2)  55 us
  transfers between devices with their start and end apart: 4, of which 3 were waited for; matrix products, arithmetic and copies ran while one was open for 44% of the time, Pallas kernels for 0%

profile of v2, /device:TPU:0, one launch (start us, length us, event | category | flops | bytes accessed | tf_op | source)
XLA Modules:
  0.0 757.2 jit_solution(9091838338459285078)
XLA Ops:
  13.8 27.5 %all-gather.7.cloned.1.call-done = f32[1,256,4,256]{3,1,0,2:T(8,128)} async-done(((f32[1,256,1,256]{3,1,0,2:T(8,128)}), f32[1,256,4,256]{3,1,0,2:T(8,128)}) %all-gather.7.cloned.1.call-update) | async-done | bytes 1048592 | tf_op jit(solution)/shard_map/all_gather | solution.py:76
  42.8 27.5 %all-gather.9.cloned.1.call-done = f32[1,256,4,256]{3,1,0,2:T(8,128)} async-done(((f32[1,256,1,256]{3,1,0,2:T(8,128)}), f32[1,256,4,256]{3,1,0,2:T(8,128)}) %all-gather.9.cloned.1.call-update) | async-done | bytes 1048592 | tf_op jit(solution)/shard_map/all_gather | solution.py:76
  71.9 78.3 %all-gather.11.cloned.1.call-done = f32[32,256,1,256]{3,1,2,0:T(8,128)} async-done(((f32[1,256,1,256]{3,1,2,0:T(8,128)}), f32[32,256,1,256]{3,1,2,0:T(8,128)}) %all-gather.11.cloned.1.call-update) | async-done | bytes 8388624 | tf_op jit(solution)/shard_map/all_gather | solution.py:16
  156.3 11.7 %custom-call.36 = f32[128,128]{1,0:T(8,128)S(1)} custom-call(f32[128,128]{1,0:T(8,128)S(1)} %copy.248), custom_call_target="Cholesky" | custom-call | tf_op jit(solution)/shard_map/cholesky/custom-call.1 | solution.py:41
  170.1 9.8 %custom-call.37 = f32[1,128,128]{1,2,0:T(8,128)S(1)} custom-call(f32[1,128,128]{2,1,0:T(8,128)S(1)} %get-tuple-element.133), custom_call_target="InvertDiagBlocksLowerTriangular" | custom-call | tf_op jit(solution)/shard_map/triangular_solve/custom-call.0 | solution.py:36
  185.6 12.6 %custom-call.38 = f32[128,128]{1,0:T(8,128)S(1)} custom-call(f32[128,128]{1,0:T(8,128)} %copy.252), custom_call_target="Cholesky" | custom-call | tf_op jit(solution)/shard_map/cholesky/custom-call.1 | solution.py:45
  200.0 10.9 %custom-call.39 = f32[1,128,128]{1,2,0:T(8,128)} custom-call(f32[1,128,128]{2,1,0:T(8,128)S(1)} %get-tuple-element.131), custom_call_target="InvertDiagBlocksLowerTriangular" | custom-call | tf_op jit(solution)/shard_map/triangular_solve/custom-call.0 | solution.py:36
  212.0 4.7 fusion.222
  283.2 3.7 fusion.112
  295.6 11.7 %custom-call.40 = f32[128,128]{1,0:T(8,128)S(1)} custom-call(f32[128,128]{1,0:T(8,128)S(1)} %slice.633), custom_call_target="Cholesky" | custom-call | tf_op jit(solution)/shard_map/cholesky/custom-call.1 | solution.py:41
  309.4 9.8 %custom-call.41 = f32[1,128,128]{1,2,0:T(8,128)S(1)} custom-call(f32[1,128,128]{2,1,0:T(8,128)S(1)} %get-tuple-element.129), custom_call_target="InvertDiagBlocksLowerTriangular" | custom-call | tf_op jit(solution)/shard_map/triangular_solve/custom-call.0 | solution.py:36
  326.2 13.2 %custom-call.42 = f32[128,128]{1,0:T(8,128)} custom-call(f32[128,128]{1,0:T(8,128)} %fusion.191), custom_call_target="Cholesky" | custom-call | tf_op jit(solution)/shard_map/cholesky/custom-call.1 | solution.py:45
  343.0 11.5 %custom-call.43 = f32[1,128,128]{1,2,0:T(8,128)} custom-call(f32[1,128,128]{2,1,0:T(8,128)} %get-tuple-element.127), custom_call_target="InvertDiagBlocksLowerTriangular" | custom-call | tf_op jit(solution)/shard_map/triangular_solve/custom-call.0 | solution.py:36
  357.7 8.9 %scatter.26 = f32[2304,2048]{1,0:T(8,128)} pad(f32[2304,256]{1,0:T(8,128)S(1)} %fusion.22, f32[]{:T(128)} %constant.301.clone.1), padding=0_0x0_1792 | pad | bytes 21233668 | tf_op jit(solution)/shard_map/scatter | solution.py:94
  367.3 3.1 fusion.29
  372.7 5.6 fusion.18
  378.6 12.2 %custom-call.44 = f32[128,128]{1,0:T(8,128)S(1)} custom-call(f32[128,128]{1,0:T(8,128)S(1)} %slice.647), custom_call_target="Cholesky" | custom-call | tf_op jit(solution)/shard_map/cholesky/custom-call.1 | solution.py:41
  392.1 9.8 %custom-call.45 = f32[1,128,128]{1,2,0:T(8,128)S(1)} custom-call(f32[1,128,128]{2,1,0:T(8,128)S(1)} %get-tuple-element.125), custom_call_target="InvertDiagBlocksLowerTriangular" | custom-call | tf_op jit(solution)/shard_map/triangular_solve/custom-call.0 | solution.py:36
  403.0 11.7 %custom-call.46 = f32[128,128]{1,0:T(8,128)S(1)} custom-call(f32[128,128]{1,0:T(8,128)S(1)} %fusion.188), custom_call_target="Cholesky" | custom-call | tf_op jit(solution)/shard_map/cholesky/custom-call.1 | solution.py:45
  416.0 9.8 %custom-call.47 = f32[1,128,128]{1,2,0:T(8,128)S(1)} custom-call(f32[1,128,128]{2,1,0:T(8,128)S(1)} %get-tuple-element.123), custom_call_target="InvertDiagBlocksLowerTriangular" | custom-call | tf_op jit(solution)/shard_map/triangular_solve/custom-call.0 | solution.py:36
  431.7 6.5 fusion.15
  438.6 11.7 %custom-call.48 = f32[128,128]{1,0:T(8,128)S(1)} custom-call(f32[128,128]{1,0:T(8,128)S(1)} %copy.304), custom_call_target="Cholesky" | custom-call | tf_op jit(solution)/shard_map/cholesky/custom-call.1 | solution.py:41
  451.6 9.8 %custom-call.49 = f32[1,128,128]{1,2,0:T(8,128)S(1)} custom-call(f32[1,128,128]{2,1,0:T(8,128)S(1)} %get-tuple-element.121), custom_call_target="InvertDiagBlocksLowerTriangular" | custom-call | tf_op jit(solution)/shard_map/triangular_solve/custom-call.0 | solution.py:36
  463.2 11.7 %custom-call.50 = f32[128,128]{1,0:T(8,128)S(1)} custom-call(f32[128,128]{1,0:T(8,128)S(1)} %copy.308), custom_call_target="Cholesky" | custom-call | tf_op jit(solution)/shard_map/cholesky/custom-call.1 | solution.py:45
  476.9 10.2 %custom-call.51 = f32[1,128,128]{1,2,0:T(8,128)S(1)} custom-call(f32[1,128,128]{2,1,0:T(8,128)S(1)} %get-tuple-element.119), custom_call_target="InvertDiagBlocksLowerTriangular" | custom-call | tf_op jit(solution)/shard_map/triangular_solve/custom-call.0 | solution.py:36
  501.0 3.3 fusion.42
  506.7 7.5 fusion.12
  514.7 11.9 %custom-call.52 = f32[128,128]{1,0:T(8,128)S(1)} custom-call(f32[128,128]{1,0:T(8,128)S(1)} %copy.321), custom_call_target="Cholesky" | custom-call | tf_op jit(solution)/shard_map/cholesky/custom-call.1 | solution.py:41
  527.8 9.8 %custom-call.53 = f32[1,128,128]{1,2,0:T(8,128)S(1)} custom-call(f32[1,128,128]{2,1,0:T(8,128)S(1)} %get-tuple-element.117), custom_call_target="InvertDiagBlocksLowerTriangular" | custom-call | tf_op jit(solution)/shard_map/triangular_solve/custom-call.0 | solution.py:36
  539.0 11.7 %custom-call.54 = f32[128,128]{1,0:T(8,128)S(1)} custom-call(f32[128,128]{1,0:T(8,128)S(1)} %copy.325), custom_call_target="Cholesky" | custom-call | tf_op jit(solution)/shard_map/cholesky/custom-call.1 | solution.py:45
  552.0 9.8 %custom-call.55 = f32[1,128,128]{1,2,0:T(8,128)S(1)} custom-call(f32[1,128,128]{2,1,0:T(8,128)S(1)} %get-tuple-element.115), custom_call_target="InvertDiagBlocksLowerTriangular" | custom-call | tf_op jit(solution)/shard_map/triangular_solve/custom-call.0 | solution.py:36
  566.0 6.8 fusion.36
  573.3 11.7 %custom-call.56 = f32[128,128]{1,0:T(8,128)S(1)} custom-call(f32[128,128]{1,0:T(8,128)S(1)} %copy.332), custom_call_target="Cholesky" | custom-call | tf_op jit(solution)/shard_map/cholesky/custom-call.1 | solution.py:41
  586.4 9.8 %custom-call.57 = f32[1,128,128]{1,2,0:T(8,128)S(1)} custom-call(f32[1,128,128]{2,1,0:T(8,128)S(1)} %get-tuple-element.113), custom_call_target="InvertDiagBlocksLowerTriangular" | custom-call | tf_op jit(solution)/shard_map/triangular_solve/custom-call.0 | solution.py:36
  597.6 11.7 %custom-call.58 = f32[128,128]{1,0:T(8,128)S(1)} custom-call(f32[128,128]{1,0:T(8,128)S(1)} %copy.336), custom_call_target="Cholesky" | custom-call | tf_op jit(solution)/shard_map/cholesky/custom-call.1 | solution.py:45
  610.7 10.0 %custom-call.59 = f32[1,128,128]{1,2,0:T(8,128)S(1)} custom-call(f32[1,128,128]{2,1,0:T(8,128)S(1)} %get-tuple-element.111), custom_call_target="InvertDiagBlocksLowerTriangular" | custom-call | tf_op jit(solution)/shard_map/triangular_solve/custom-call.0 | solution.py:36
  623.6 7.1 fusion.44
  631.1 11.7 %custom-call.60 = f32[128,128]{1,0:T(8,128)S(1)} custom-call(f32[128,128]{1,0:T(8,128)S(1)} %copy.345), custom_call_target="Cholesky" | custom-call | tf_op jit(solution)/shard_map/cholesky/custom-call.1 | solution.py:41
  644.2 10.0 %custom-call.61 = f32[1,128,128]{1,2,0:T(8,128)S(1)} custom-call(f32[1,128,128]{2,1,0:T(8,128)S(1)} %get-tuple-element.109), custom_call_target="InvertDiagBlocksLowerTriangular" | custom-call | tf_op jit(solution)/shard_map/triangular_solve/custom-call.0 | solution.py:36
  655.5 11.7 %custom-call.62 = f32[128,128]{1,0:T(8,128)S(1)} custom-call(f32[128,128]{1,0:T(8,128)S(1)} %fusion.176), custom_call_target="Cholesky" | custom-call | tf_op jit(solution)/shard_map/cholesky/custom-call.1 | solution.py:45
  668.5 9.8 %custom-call.63 = f32[1,128,128]{1,2,0:T(8,128)S(1)} custom-call(f32[1,128,128]{2,1,0:T(8,128)S(1)} %get-tuple-element.107), custom_call_target="InvertDiagBlocksLowerTriangular" | custom-call | tf_op jit(solution)/shard_map/triangular_solve/custom-call.0 | solution.py:36
  681.2 6.3 fusion.49
  687.9 11.7 %custom-call.64 = f32[128,128]{1,0:T(8,128)S(1)} custom-call(f32[128,128]{1,0:T(8,128)S(1)} %copy.355), custom_call_target="Cholesky" | custom-call | tf_op jit(solution)/shard_map/cholesky/custom-call.1 | solution.py:41
  700.9 9.8 %custom-call.65 = f32[1,128,128]{1,2,0:T(8,128)S(1)} custom-call(f32[1,128,128]{2,1,0:T(8,128)S(1)} %get-tuple-element.105), custom_call_target="InvertDiagBlocksLowerTriangular" | custom-call | tf_op jit(solution)/shard_map/triangular_solve/custom-call.0 | solution.py:36
  712.2 11.7 %custom-call.66 = f32[128,128]{1,0:T(8,128)S(1)} custom-call(f32[128,128]{1,0:T(8,128)S(1)} %broadcast_multiply_fusion.1), custom_call_target="Cholesky" | custom-call | tf_op jit(solution)/shard_map/cholesky/custom-call.1 | solution.py:45
  725.2 9.9 %custom-call.67 = f32[1,128,128]{1,2,0:T(8,128)S(1)} custom-call(f32[1,128,128]{2,1,0:T(8,128)S(1)} %get-tuple-element.103), custom_call_target="InvertDiagBlocksLowerTriangular" | custom-call | tf_op jit(solution)/shard_map/triangular_solve/custom-call.0 | solution.py:36
  737.4 3.9 constant_dynamic-slice_fusion.3
  741.3 2.9 copy.362
  (374 shorter events, 187.6 us)
Async XLA Ops:
  6.5 34.7 %all-gather.7.cloned.1.call-start = ((), (), s32[]{:S(2)}) async-start(), calls=%async_computation | async-start | bytes 1310720 | tf_op jit(solution)/shard_map/all_gather | solution.py:76
  10.5 59.8 %all-gather.9.cloned.1.call-start = ((), (), s32[]{:S(2)}) async-start(), calls=%async_computation.1 | async-start | bytes 1310720 | tf_op jit(solution)/shard_map/all_gather | solution.py:76
  11.2 138.9 %all-gather.11.cloned.1.call-start = ((), (), s32[]{:S(2)}) async-start(), calls=%async_computation.2 | async-start | bytes 8650752 | tf_op jit(solution)/shard_map/all_gather | solution.py:16
  12.0 477.3 %all-gather.13.cloned.1.call-start = ((), (), s32[]{:S(2)}) async-start(), calls=%async_computation.3 | async-start | bytes 8650752 | tf_op jit(solution)/shard_map/all_gather | solution.py:16
  13.6 280.2 %copy-start.31 = (pred[256,256]{0,1:T(8,128)(4,1)}, pred[256,256]{0,1:T(8,128)(4,1)S(1)}, u32[]{:S(2)}) copy-start(pred[256,256]{0,1:T(8,128)(4,1)S(1)} %copy.275) | copy-start | bytes 196612
  13.8 280.0 %copy-start.33 = (pred[256,256]{1,0:T(8,128)(4,1)}, pred[256,256]{1,0:T(8,128)(4,1)S(1)}, u32[]{:S(2)}) copy-start(pred[256,256]{1,0:T(8,128)(4,1)S(1)} %copy.273) | copy-start | bytes 196612
  259.0 8.3 %copy-start.14 = (f32[1,256,1,256]{3,1,2,0:T(8,128)S(1)}, f32[1,256,1,256]{3,1,2,0:T(8,128)}, u32[]{:S(2)}) copy-start(f32[1,256,1,256]{3,1,2,0:T(8,128)} %get-tuple-element.147) | copy-start | bytes 786436
  267.5 7.2 copy-start.4
  267.5 11.4 %copy-start.22 = (f32[1,256,1,256]{1,3,2,0:T(8,128)S(1)}, f32[1,256,1,256]{1,3,2,0:T(8,128)}, u32[]{:S(2)}) copy-start(f32[1,256,1,256]{1,3,2,0:T(8,128)} %copy.407) | copy-start | bytes 786436
  269.4 9.5 %copy-start.3 = (f32[2048,256]{0,1:T(8,128)S(1)}, f32[2048,256]{0,1:T(8,128)}, u32[]{:S(2)}) copy-start(f32[2048,256]{0,1:T(8,128)} %bitcast_dynamic-update-slice_fusion.28) | copy-start | bytes 6291460
  269.4 9.6 %copy-start.20 = (f32[1,256,1,256]{1,3,2,0:T(8,128)S(1)}, f32[1,256,1,256]{1,3,2,0:T(8,128)}, u32[]{:S(2)}) copy-start(f32[1,256,1,256]{1,3,2,0:T(8,128)} %copy.389) | copy-start | bytes 786436
  271.2 7.7 %copy-start.21 = (f32[1,256,1,256]{1,3,2,0:T(8,128)S(1)}, f32[1,256,1,256]{1,3,2,0:T(8,128)}, u32[]{:S(2)}) copy-start(f32[1,256,1,256]{1,3,2,0:T(8,128)} %copy.390) | copy-start | bytes 786436
  273.0 6.0 copy-start.19
  274.7 4.4 copy-start.17
  275.7 3.4 copy-start.18
  276.7 2.4 copy-start.16
  277.7 1.5 copy-start.7
  278.9 1.0 copy-start.15
  279.0 1.7 copy-start.2
  279.2 3.9 copy-start.41
  280.8 1.3 copy-start.5
  282.0 1.2 copy-start.8
  283.2 3.7 copy-start.36
  283.2 3.7 copy-start.37
  283.2 3.7 copy-start.40
  290.0 1.3 copy-start
  357.7 9.2 %copy-start.35 = (f32[128,128]{0,1:T(8,128)S(1)}, f32[128,128]{0,1:T(8,128)}, u32[]{:S(2)}) copy-start(f32[128,128]{0,1:T(8,128)} %fusion.94) | copy-start | bytes 196612
  357.7 9.5 %copy-start.1 = (f32[2048,256]{0,1:T(8,128)S(1)}, f32[2048,256]{0,1:T(8,128)}, u32[]{:S(2)}) copy-start(f32[2048,256]{0,1:T(8,128)} %copy-done) | copy-start | bytes 6291460
  357.7 9.6 %copy-start.43 = (f32[128,128]{1,0:T(8,128)S(1)}, f32[128,128]{1,0:T(8,128)}, u32[]{:S(2)}) copy-start(f32[128,128]{1,0:T(8,128)} %copy.280) | copy-start | bytes 196612
  366.7 3.8 copy-start.38
  366.7 3.8 copy-start.39
  366.7 3.8 copy-start.42
  370.4 2.3 copy-start.6
  372.7 5.8 copy-start.32
  372.7 5.8 copy-start.34
  429.7 2.1 copy-start.9
  501.0 3.3 copy-start.10
  501.0 3.3 copy-start.24
  501.0 3.4 copy-start.25
  501.0 3.4 copy-start.23
  504.3 1.1 copy-start.44
  504.3 1.1 copy-start.45
  514.3 48.2 %copy-start.28 = (f32[256,256]{0,1:T(8,128)S(1)}, f32[256,256]{0,1:T(8,128)}, u32[]{:S(2)}) copy-start(f32[256,256]{0,1:T(8,128)} %get-tuple-element.175) | copy-start | bytes 786436
  572.9 48.5 %copy-start.13 = (f32[1,256,1,256]{3,1,2,0:T(8,128)S(1)}, f32[1,256,1,256]{3,1,2,0:T(8,128)}, u32[]{:S(2)}) copy-start(f32[1,256,1,256]{3,1,2,0:T(8,128)} %get-tuple-element.139) | copy-start | bytes 786436
  573.0 48.5 %copy-start.12 = (f32[1,256,1,256]{3,1,2,0:T(8,128)S(1)}, f32[1,256,1,256]{3,1,2,0:T(8,128)}, u32[]{:S(2)}) copy-start(f32[1,256,1,256]{3,1,2,0:T(8,128)} %get-tuple-element.138) | copy-start | bytes 786436
  621.5 2.1 copy-start.27
  630.7 48.3 %copy-start.11 = (f32[1,256,1,256]{3,1,2,0:T(8,128)S(1)}, f32[1,256,1,256]{3,1,2,0:T(8,128)}, u32[]{:S(2)}) copy-start(f32[1,256,1,256]{3,1,2,0:T(8,128)} %get-tuple-element.137) | copy-start | bytes 786436
  655.4 25.7 %copy-start.26 = (f32[256,256]{0,1:T(8,128)S(1)}, f32[256,256]{0,1:T(8,128)}, u32[]{:S(2)}) copy-start(f32[256,256]{0,1:T(8,128)} %get-tuple-element.173) | copy-start | bytes 786436
  (2 other events, 1.4 us)
Sparse Core Ops, SparseCore 0:
  10.6 30.6 all-gather.6
  42.8 27.4 all-gather.8
  73.2 76.8 all-gather.10
  153.0 76.2 all-gather.12

commit v3 on v2

--- a/solution.py
+++ b/solution.py
@@ -32,8 +32,18 @@
 
 
 def lower_inverse(lower):
-    eye = jnp.eye(lower.shape[0], dtype=lower.dtype)
-    return lax.linalg.triangular_solve(lower, eye, left_side=True, lower=True)
+    size = lower.shape[0]
+    eye = jnp.eye(size, dtype=lower.dtype)
+    diag = jnp.diagonal(lower)
+    strict = jnp.tril(jnp.ones((size, size), jnp.bool_), -1)
+    power = jnp.where(strict, -lower / diag[:, None], 0.0)
+    product = eye + power
+    span = 2
+    while span < size:
+        power = mm(power, power)
+        product = mm(product, eye + power)
+        span *= 2
+    return product / diag[None, :]
 
 
 def factor_diag(diag):

time: 769 us -> 635 us (0.83)
  other arithmetic: 395 us -> 227 us
  matrix products: 81 us -> 113 us
    another operation x34 -> x2, other arithmetic: 176 us -> 1.72 us  [the longest x32 175 us: lower_inverse(): return lax.linalg.triangular_solve(lower, eye, left_side=True, lower=True)]
    dot_general x47 -> x239, matrix products: 74.3 us -> 113 us  [mm(): return jnp.dot(a, b, precision=HIGHEST, preferred_element_type=jnp.float32)]
    gather x0 -> x16, local copies, waits for them, and re-layouts: none -> 21.7 us  [lower_inverse(): diag = jnp.diagonal(lower)]
    unnamed x155 -> x145, local copies, waits for them, and re-layouts: 78.9 us -> 67.4 us
    select_n x0 -> x16, other arithmetic: none -> 9.88 us  [the longest x8 4.97 us: factor_diag(): jnp.tril(lax.linalg.cholesky(diag[:half, :half], symmetrize_input=False))]
  transfers between devices with their start and end apart: 4 -> 4, of which waited for: 3 -> 3; matrix products, arithmetic and copies ran while one was open for 44% -> 41% of each run, Pallas kernels for 0% -> 0%
where the time goes in v3:
time: 635 us; the launch traced here: 624 us
  other arithmetic  227 us (36%)
  local copies, waits for them, and re-layouts  134 us (21%)
  waiting for transfers between devices  133 us (21%)
  matrix products  113 us (18%)
  between operations  16.8 us (3%)
    dot_general x239, matrix products, mm(): return jnp.dot(a, b, precision=HIGHEST, preferred_element_type=jnp.float32)  113 us
    another operation x24, other arithmetic, factor_diag(): lax.linalg.cholesky(diag[:half, :half], symmetrize_input=False)  100 us
    another operation x24, other arithmetic, factor_diag(): l11 = jnp.tril(lax.linalg.cholesky(s11, symmetrize_input=True))  99.2 us
    all_gather x2, waiting for transfers between devices, separator_tiles(): lax.all_gather(sep_local[:, :, t, :], ('row', 'col'), axis=0)  77.4 us
    unnamed x145, local copies, waits for them, and re-layouts  67.4 us
    all_gather x2, waiting for transfers between devices, shards(): lax.all_gather(working[tail_first:, :, t, :], 'col', axis=2)  53.8 us
    gather x16, local copies, waits for them, and re-layouts, lower_inverse(): diag = jnp.diagonal(lower)  21.7 us
  transfers between devices with their start and end apart: 4, of which 3 were waited for; matrix products, arithmetic and copies ran while one was open for 41% of the time, Pallas kernels for 0%

profile of v3, /device:TPU:0, one launch (start us, length us, event | category | flops | bytes accessed | tf_op | source)
XLA Modules:
  0.0 624.1 jit_solution(17569513424520517133)
XLA Ops:
  15.0 26.3 %all-gather.7.cloned.1.call-done = f32[1,256,4,256]{3,1,0,2:T(8,128)} async-done(((f32[1,256,1,256]{3,1,0,2:T(8,128)}), f32[1,256,4,256]{3,1,0,2:T(8,128)}) %all-gather.7.cloned.1.call-update) | async-done | bytes 1048592 | tf_op jit(solution)/shard_map/all_gather | solution.py:86
  42.8 27.5 %all-gather.9.cloned.1.call-done = f32[1,256,4,256]{3,1,0,2:T(8,128)} async-done(((f32[1,256,1,256]{3,1,0,2:T(8,128)}), f32[1,256,4,256]{3,1,0,2:T(8,128)}) %all-gather.9.cloned.1.call-update) | async-done | bytes 1048592 | tf_op jit(solution)/shard_map/all_gather | solution.py:86
  70.3 2.5 copy.317
  72.8 77.4 %all-gather.11.cloned.1.call-done = f32[32,256,1,256]{3,1,2,0:T(8,128)} async-done(((f32[1,256,1,256]{3,1,2,0:T(8,128)}), f32[32,256,1,256]{3,1,2,0:T(8,128)}) %all-gather.11.cloned.1.call-update) | async-done | bytes 8388624 | tf_op jit(solution)/shard_map/all_gather | solution.py:16
  150.2 2.5 fusion.271
  154.0 11.7 %custom-call.50 = f32[128,128]{1,0:T(8,128)S(1)} custom-call(f32[128,128]{1,0:T(8,128)S(1)} %copy.248), custom_call_target="Cholesky" | custom-call | tf_op jit(solution)/shard_map/cholesky/custom-call.1 | solution.py:51
  172.8 11.7 %custom-call.51 = f32[128,128]{1,0:T(8,128)S(1)} custom-call(f32[128,128]{1,0:T(8,128)S(1)} %copy.252), custom_call_target="Cholesky" | custom-call | tf_op jit(solution)/shard_map/cholesky/custom-call.1 | solution.py:55
  191.8 4.6 fusion.270
  199.9 1.8 copy.405
  201.8 1.8 copy.406
  205.4 1.8 copy.408
  207.2 1.8 copy.409
  217.9 1.8 copy.414
  228.6 1.8 copy.399
  233.0 1.8 copy.402
  257.3 3.6 fusion.80
  262.4 2.1 convolution_subtract_fusion
  267.1 12.1 %custom-call.52 = f32[128,128]{1,0:T(8,128)S(1)} custom-call(f32[128,128]{1,0:T(8,128)S(1)} %slice.663), custom_call_target="Cholesky" | custom-call | tf_op jit(solution)/shard_map/cholesky/custom-call.1 | solution.py:51
  285.5 11.7 %custom-call.53 = f32[128,128]{1,0:T(8,128)S(1)} custom-call(f32[128,128]{1,0:T(8,128)S(1)} %fusion.226), custom_call_target="Cholesky" | custom-call | tf_op jit(solution)/shard_map/cholesky/custom-call.1 | solution.py:55
  302.9 4.6 fusion.29
  307.6 8.9 %scatter.26 = f32[2304,2048]{1,0:T(8,128)} pad(f32[2304,256]{1,0:T(8,128)S(1)} %fusion.22, f32[]{:T(128)} %constant.368.clone.1), padding=0_0x0_1792 | pad | bytes 21233668 | tf_op jit(solution)/shard_map/scatter | solution.py:104
  318.8 5.5 fusion.18
  324.6 11.9 %custom-call.54 = f32[128,128]{1,0:T(8,128)S(1)} custom-call(f32[128,128]{1,0:T(8,128)S(1)} %slice.677), custom_call_target="Cholesky" | custom-call | tf_op jit(solution)/shard_map/cholesky/custom-call.1 | solution.py:51
  342.4 11.7 %custom-call.55 = f32[128,128]{1,0:T(8,128)S(1)} custom-call(f32[128,128]{1,0:T(8,128)S(1)} %fusion.225), custom_call_target="Cholesky" | custom-call | tf_op jit(solution)/shard_map/cholesky/custom-call.1 | solution.py:55
  360.2 2.7 fusion.34
  365.0 6.4 %fusion.15 = f32[1536,256]{0,1:T(8,128)S(1)} fusion(f32[1536,256]{0,1:T(8,128)S(1)} %copy-done.10, f32[2304,2048]{1,0:T(8,128)} %fusion.28), kind=kOutput, calls=%fused_computation.29 | convolution fusion | flops 3624271872 | bytes 8650752 | tf_op jit(solution)/shard_map/dot_general | solution.py:10
  371.9 11.7 %custom-call.56 = f32[128,128]{1,0:T(8,128)S(1)} custom-call(f32[128,128]{1,0:T(8,128)S(1)} %copy.304), custom_call_target="Cholesky" | custom-call | tf_op jit(solution)/shard_map/cholesky/custom-call.1 | solution.py:51
  390.4 11.7 %custom-call.57 = f32[128,128]{1,0:T(8,128)S(1)} custom-call(f32[128,128]{1,0:T(8,128)S(1)} %copy.308), custom_call_target="Cholesky" | custom-call | tf_op jit(solution)/shard_map/cholesky/custom-call.1 | solution.py:55
  407.7 2.3 fusion.42
  410.1 2.9 fusion.269
  414.9 2.3 fusion.33
  420.5 7.9 %fusion.12 = f32[1280,256]{0,1:T(8,128)S(1)} fusion(f32[1280,256]{0,1:T(8,128)} %get-tuple-element.143, f32[2304,2048]{1,0:T(8,128)} %fusion.33), kind=kOutput, calls=%fused_computation.28 | convolution fusion | flops 4026859520 | bytes 8912896 | tf_op jit(solution)/shard_map/dot_general | solution.py:10
  428.8 12.1 %custom-call.58 = f32[128,128]{1,0:T(8,128)S(1)} custom-call(f32[128,128]{1,0:T(8,128)S(1)} %copy.321), custom_call_target="Cholesky" | custom-call | tf_op jit(solution)/shard_map/cholesky/custom-call.1 | solution.py:51
  447.2 11.7 %custom-call.59 = f32[128,128]{1,0:T(8,128)S(1)} custom-call(f32[128,128]{1,0:T(8,128)S(1)} %copy.325), custom_call_target="Cholesky" | custom-call | tf_op jit(solution)/shard_map/cholesky/custom-call.1 | solution.py:55
  465.1 1.9 fusion.56
  468.1 2.1 fusion.41
  470.2 7.0 %fusion.36 = f32[1024,256]{1,0:T(8,128)S(1)} fusion(f32[2304,2048]{1,0:T(8,128)} %fusion.41, f32[256,256]{1,0:T(8,128)S(1)} %copy.425, f32[256,256]{1,0:T(8,128)S(1)} %copy-done.11, f32[256,256]{1,0:T(8,128)S(1)} %get-tuple-element.111, f32[256,256]{1,0:T(8,128)S(1)} %get-tuple-element.112), kind=kOutput, calls=%fused_computation.167 | convolution fusion | flops 4027580416 | bytes 8650752 | tf_op jit(solution)/shard_map/dot_general | solution.py:10
  477.5 11.7 %custom-call.60 = f32[128,128]{1,0:T(8,128)S(1)} custom-call(f32[128,128]{1,0:T(8,128)S(1)} %copy.332), custom_call_target="Cholesky" | custom-call | tf_op jit(solution)/shard_map/cholesky/custom-call.1 | solution.py:51
  495.6 11.7 %custom-call.61 = f32[128,128]{1,0:T(8,128)S(1)} custom-call(f32[128,128]{1,0:T(8,128)S(1)} %copy.336), custom_call_target="Cholesky" | custom-call | tf_op jit(solution)/shard_map/cholesky/custom-call.1 | solution.py:55
  515.6 7.2 %fusion.44 = f32[768,256]{0,1:T(8,128)S(1)} fusion(f32[2304,2048]{1,0:T(8,128)} %fusion.55, f32[256,256]{0,1:T(8,128)S(1)} %copy-done.35, f32[256,256]{0,1:T(8,128)S(1)} %bitcast.459, f32[256,256]{0,1:T(8,128)S(1)} %bitcast.458), kind=kOutput, calls=%fused_computation.175 | convolution fusion | flops 3624468480 | bytes 7864320 | tf_op jit(solution)/shard_map/dot_general | solution.py:10
  523.1 11.7 %custom-call.62 = f32[128,128]{1,0:T(8,128)S(1)} custom-call(f32[128,128]{1,0:T(8,128)S(1)} %copy.345), custom_call_target="Cholesky" | custom-call | tf_op jit(solution)/shard_map/cholesky/custom-call.1 | solution.py:51
  541.2 11.7 %custom-call.63 = f32[128,128]{1,0:T(8,128)S(1)} custom-call(f32[128,128]{1,0:T(8,128)S(1)} %fusion.221), custom_call_target="Cholesky" | custom-call | tf_op jit(solution)/shard_map/cholesky/custom-call.1 | solution.py:55
  560.7 5.9 fusion.49
  567.0 11.7 %custom-call.64 = f32[128,128]{1,0:T(8,128)S(1)} custom-call(f32[128,128]{1,0:T(8,128)S(1)} %copy.355), custom_call_target="Cholesky" | custom-call | tf_op jit(solution)/shard_map/cholesky/custom-call.1 | solution.py:51
  585.2 11.7 %custom-call.65 = f32[128,128]{1,0:T(8,128)S(1)} custom-call(f32[128,128]{1,0:T(8,128)S(1)} %broadcast_multiply_fusion.1), custom_call_target="Cholesky" | custom-call | tf_op jit(solution)/shard_map/cholesky/custom-call.1 | solution.py:55
  604.0 3.9 constant_dynamic-slice_fusion.3
  607.9 2.9 copy.362
  612.2 1.9 copy.364
  (534 shorter events, 183.5 us)
Async XLA Ops:
  6.5 34.7 %all-gather.7.cloned.1.call-start = ((), (), s32[]{:S(2)}) async-start(), calls=%async_computation | async-start | bytes 1310720 | tf_op jit(solution)/shard_map/all_gather | solution.py:86
  10.5 59.8 %all-gather.9.cloned.1.call-start = ((), (), s32[]{:S(2)}) async-start(), calls=%async_computation.1 | async-start | bytes 1310720 | tf_op jit(solution)/shard_map/all_gather | solution.py:86
  11.2 138.9 %all-gather.11.cloned.1.call-start = ((), (), s32[]{:S(2)}) async-start(), calls=%async_computation.2 | async-start | bytes 8650752 | tf_op jit(solution)/shard_map/all_gather | solution.py:16
  12.0 398.1 %all-gather.13.cloned.1.call-start = ((), (), s32[]{:S(2)}) async-start(), calls=%async_computation.3 | async-start | bytes 8650752 | tf_op jit(solution)/shard_map/all_gather | solution.py:16
  171.1 13.4 %copy-start.36 = (f32[128,128]{1,0:T(8,128)}, f32[128,128]{1,0:T(8,128)S(1)}, u32[]{:S(2)}) copy-start(f32[128,128]{1,0:T(8,128)S(1)} %convolution_divide_fusion.15) | copy-start | bytes 196612
  233.0 10.7 %copy-start.15 = (f32[1,256,1,256]{3,1,2,0:T(8,128)S(1)}, f32[1,256,1,256]{3,1,2,0:T(8,128)}, u32[]{:S(2)}) copy-start(f32[1,256,1,256]{3,1,2,0:T(8,128)} %get-tuple-element.114) | copy-start | bytes 786436
  244.5 6.6 %copy-start.27 = (f32[1,256,1,256]{1,3,2,0:T(8,128)S(1)}, f32[1,256,1,256]{1,3,2,0:T(8,128)}, u32[]{:S(2)}) copy-start(f32[1,256,1,256]{1,3,2,0:T(8,128)} %copy.408) | copy-start | bytes 786436
  244.5 6.6 %copy-start.22 = (f32[1,256,1,256]{1,3,2,0:T(8,128)S(1)}, f32[1,256,1,256]{1,3,2,0:T(8,128)}, u32[]{:S(2)}) copy-start(f32[1,256,1,256]{1,3,2,0:T(8,128)} %copy.409) | copy-start | bytes 786436
  244.5 6.7 %copy-start.5 = (f32[1792,256]{0,1:T(8,128)S(1)}, f32[1792,256]{0,1:T(8,128)}, u32[]{:S(2)}) copy-start(f32[1792,256]{0,1:T(8,128)} %bitcast_dynamic-update-slice_fusion.14) | copy-start | bytes 5505028
  244.5 6.7 %copy-start.31 = (f32[1,256,1,256]{1,3,2,0:T(8,128)S(1)}, f32[1,256,1,256]{1,3,2,0:T(8,128)}, u32[]{:S(2)}) copy-start(f32[1,256,1,256]{1,3,2,0:T(8,128)} %copy.411) | copy-start | bytes 786436
  244.5 6.7 %copy-start.32 = (f32[1,256,1,256]{1,3,2,0:T(8,128)S(1)}, f32[1,256,1,256]{1,3,2,0:T(8,128)}, u32[]{:S(2)}) copy-start(f32[1,256,1,256]{1,3,2,0:T(8,128)} %copy.412) | copy-start | bytes 786436
  246.8 4.5 copy-start.28
  247.8 3.5 copy-start.23
  248.9 2.5 copy-start.17
  249.9 1.7 copy-start.4
  249.9 1.7 copy-start.29
  251.1 1.1 copy-start.30
  251.1 1.1 copy-start.24
  251.2 1.1 copy-start.18
  251.2 1.1 copy-start.19
  251.3 1.2 copy-start.16
  251.3 1.7 copy-start.8
  251.3 1.7 copy-start.25
  251.4 1.7 copy-start.26
  251.6 1.5 copy-start.20
  252.2 1.2 copy-start.21
  253.0 4.3 copy-start.37
  253.5 1.2 copy-start.6
  254.7 1.2 copy-start.9
  255.9 1.4 copy-start.2
  257.3 3.6 copy-start.40
  260.8 1.6 copy-start.3
  262.4 3.6 copy-start.38
  262.4 3.6 copy-start.39
  264.6 1.4 copy-start
  316.5 2.3 copy-start.7
  363.0 2.1 copy-start.10
  414.9 3.0 copy-start.33
  414.9 4.6 copy-start.1
  467.0 3.2 copy-start.11
  510.8 3.3 copy-start.14
  511.2 3.1 copy-start.13
  513.3 2.3 copy-start.35
  555.5 4.0 copy-start.12
  557.4 3.2 copy-start.34
Sparse Core Ops, SparseCore 0:
  10.6 30.6 all-gather.6
  42.8 27.4 all-gather.8
  73.2 76.8 all-gather.10
  153.0 76.3 all-gather.12
